TPU v7x, 256 devices: a whole 4x4x8 slice. The times are simulated.
256 devices in a mesh: head: 8 (over x_hi, y), inner: 2 (over x_lo), outer: 16 (over z, core).
Axes of the slice: x: 4 (x_hi: 2, x_lo: 2; x = x_hi * 2 + x_lo), y: 4, z: 8, core: 2. Of those that a mesh axis runs over, the one named last changes fastest.
Arguments:
- query_nope: bfloat16 [4096, 8192], P(('inner', 'outer'), 'head'), may hold values from -6 to 6
- query_rope: bfloat16 [4096, 4096], P(('inner', 'outer'), 'head'), may hold values from -256 to 256
- latent: bfloat16 [4096, 512], P(('inner', 'outer')), may hold values from -6 to 6
- key_rope: bfloat16 [4096, 64], P(('inner', 'outer')), may hold values from -4 to 4
- key_up: bfloat16 [512, 8192], P(None, 'head'), may hold values from -0.25 to 0.25
- value_up: bfloat16 [512, 8192], P(None, 'head'), may hold values from -0.25 to 0.25
- latent_out: bfloat16 [4096, 32768], P(('inner', 'outer'), 'head'), may hold values from -3 to 3
- out_grad: bfloat16 [4096, 8192], P(('inner', 'outer'), 'head'), may hold values from -6 to 6
- logsum: float32 [4096, 64], P(('inner', 'outer'), 'head'), may hold values from 0 to 5000
- block_order: int32 [64], replicated, may hold values from 0 to 63, as said below
Outputs:
- d_query_nope: bfloat16 [4096, 8192], P(('inner', 'outer'), 'head')
- d_query_rope: bfloat16 [4096, 4096], P(('inner', 'outer'), 'head')
- d_latent: bfloat16 [4096, 512], P(('inner', 'outer'))
- d_key_rope: bfloat16 [4096, 64], P(('inner', 'outer'))
- d_key_up: float32 [512, 8192], P(('inner', 'outer'), 'head')
- d_value_up: float32 [512, 8192], P(('inner', 'outer'), 'head')
Inputs may be any that keep to these rules, and one draw needn't show every extreme that they name: `block_order`: stored blocks 2 r and 2 r + 1 hold sequence blocks c and 63 - c for some c, in either order; every sequence block is held once.
All inputs are finite; a program needn't handle non-finite values.
Results may differ from a plain program's by a relative error of at most 0.0085.
The roundings to bfloat16 on the way count: a program that leaves them out, or rounds other values in their place, can miss the bound.
Values may be sent and summed in bfloat16 or wider, within the bound.
No kernel may reach another device: no remote copies, remote signals or barrier semaphores. Data moves between devices by JAX's collectives and lax.ppermute only.
A program may use at most 128 MiB of HBM per device.

v0:
```python
import functools

import jax
import jax.numpy as jnp
from jax import lax
from jax.sharding import PartitionSpec as P

LATENT = 512
ROPE_DIM = 64
NOPE_DIM = 128
VALUE_DIM = 128


def split_up(shard, dim, count):
    shape = shard.shape
    pieces = shard.reshape(*shape[:dim], count, shape[dim] // count, *shape[dim + 1 :])
    return jnp.moveaxis(pieces, dim, 0)


def sum_packed(arrays, axis, dims):
    count = lax.axis_size(axis)
    pieces = [split_up(a, dim, count) for a, dim in zip(arrays, dims)]
    lines = jnp.concatenate([b.reshape(count, -1) for b in pieces], axis=1)
    width = max(16, -(-lines.shape[1] // 1024) * 8)
    lines = jnp.pad(lines, ((0, 0), (0, width * 128 - lines.shape[1]))).reshape(-1, 128)
    ravelled, at, gathered = (lax.psum_scatter(lines, axis, tiled=True).reshape(-1), 0, [])
    for b in pieces:
        part = b[0]
        gathered.append(ravelled[at : at + part.size].reshape(part.shape))
        at += part.size
    return tuple(gathered)


def sent_to_all(shard, axis):
    copies = jnp.broadcast_to(shard, (lax.axis_size(axis), *shard.shape))
    return lax.all_to_all(copies, axis, split_axis=0, concat_axis=0, tiled=True)


def of_everyone(shard, axis):
    everything = sent_to_all(shard, axis)
    return jnp.sum(everything, axis=0)


def in_one(arrays, axis):
    ends = [0]
    for a in arrays:
        ends.append(ends[-1] + a.size)
    subtotal = of_everyone(jnp.concatenate([a.ravel() for a in arrays]), axis)
    return tuple((subtotal[b:e].reshape(a.shape) for a, b, e in zip(arrays, ends, ends[1:])))


def side_by_side(arrays, axis, dim, along):
    ends, at = ([], 0)
    for a in arrays[:-1]:
        at += a.shape[along]
        ends.append(at)
    both = jnp.concatenate(arrays, axis=along)
    return tuple(
        jnp.split(lax.psum_scatter(both, axis, scatter_dimension=dim, tiled=True), ends, axis=along)
    )


def key_positions(block_order, first_row, length, block_size):
    indices = first_row + lax.iota(jnp.int32, length)
    owners = indices // block_size
    lookup = lax.iota(jnp.int32, block_order.shape[0])
    picked = (owners[:, None] == lookup[None, :]).astype(jnp.int32)
    return jnp.sum(picked * block_order[None, :], axis=1) * block_size + indices % block_size


def contract_last(first_op, second_op):
    return lax.dot_general(
        first_op, second_op, (((1,), (1,)), ((), ())), preferred_element_type=jnp.float32
    )


def contract_first(first_op, second_op):
    return lax.dot_general(
        first_op, second_op, (((0,), (0,)), ((), ())), preferred_element_type=jnp.float32
    )


def scaled_scores(queries, lat_keys, rope_keys):
    factor = float(NOPE_DIM + ROPE_DIM) ** (-0.5)
    return (contract_last(lat_keys, queries[0]) + contract_last(rope_keys, queries[1])) * factor


def unchanged(current):
    return current


def grad_update(carried, queries, lat_keys, rope_keys, positions):
    factor = float(NOPE_DIM + ROPE_DIM) ** (-0.5)
    scores = scaled_scores(queries, lat_keys, rope_keys)
    visible = positions[:, None] <= queries[2][None, :]
    weights = jnp.where(
        visible, jnp.exp(jnp.where(visible, scores - queries[5][None, :], 0.0)), 0.0
    )
    dprobs = contract_last(lat_keys, queries[3])
    dscore = (weights * (dprobs - queries[4][None, :]) * factor).astype(jnp.bfloat16)
    rounded = weights.astype(jnp.bfloat16)
    return (
        carried[0] + contract_first(dscore, lat_keys),
        carried[1] + contract_first(dscore, rope_keys),
        carried[2]
        + jnp.dot(dscore, queries[0], preferred_element_type=jnp.float32)
        + jnp.dot(rounded, queries[3], preferred_element_type=jnp.float32),
        carried[3] + jnp.dot(dscore, queries[1], preferred_element_type=jnp.float32),
    )


def single_block(carried, queries, lat_keys, rope_keys, positions, offset, block_size):
    part_lat = lax.dynamic_slice_in_dim(lat_keys, offset, block_size, 0)
    part_rope = lax.dynamic_slice_in_dim(rope_keys, offset, block_size, 0)
    part_pos = lax.dynamic_slice_in_dim(positions, offset, block_size, 0)
    sum_lat = lax.dynamic_slice_in_dim(carried[2], offset, block_size, 0)
    sum_rope = lax.dynamic_slice_in_dim(carried[3], offset, block_size, 0)
    result = grad_update(
        (carried[0], carried[1], sum_lat, sum_rope), queries, part_lat, part_rope, part_pos
    )
    return (
        result[0],
        result[1],
        lax.dynamic_update_slice_in_dim(carried[2], result[2], offset, 0),
        lax.dynamic_update_slice_in_dim(carried[3], result[3], offset, 0),
    )


def shard_grads(query_pairs, query_grads, lat_keys, rope_keys, positions):
    block_size = lat_keys.shape[0] // 2
    key_lat = jnp.zeros(lat_keys.shape, jnp.float32)
    key_rope_acc = jnp.zeros(rope_keys.shape, jnp.float32)
    updated = []
    for target in range(2):
        queries = query_pairs[target]
        latest = queries[2][-1]
        first_seen = positions[0] <= latest
        second_seen = positions[block_size] <= latest
        branch_index = first_seen.astype(jnp.int32) + second_seen.astype(jnp.int32)
        offset = jnp.where(first_seen, 0, block_size).astype(jnp.int32)
        whole = functools.partial(
            grad_update,
            queries=queries,
            lat_keys=lat_keys,
            rope_keys=rope_keys,
            positions=positions,
        )
        single = functools.partial(
            single_block,
            queries=queries,
            lat_keys=lat_keys,
            rope_keys=rope_keys,
            positions=positions,
            offset=offset,
            block_size=block_size,
        )
        carried = lax.switch(
            branch_index,
            [unchanged, single, whole],
            (query_grads[target][0], query_grads[target][1], key_lat, key_rope_acc),
        )
        updated.append((carried[0], carried[1]))
        key_lat, key_rope_acc = (carried[2], carried[3])
    return (tuple(updated), (key_lat, key_rope_acc))


def local(
    query_nope,
    query_rope,
    latent,
    key_rope,
    key_up,
    value_up,
    latent_out,
    out_grad,
    logsum,
    block_order,
):
    tokens = query_nope.shape[0]
    head_count = query_nope.shape[1] // NOPE_DIM
    block_size = tokens // 2
    flat_rows = block_size * head_count
    nope_heads = query_nope.reshape(tokens, head_count, NOPE_DIM)
    rope_heads = query_rope.reshape(tokens, head_count, ROPE_DIM)
    saved = latent_out.reshape(tokens, head_count, LATENT)
    upstream = out_grad.reshape(tokens, head_count, VALUE_DIM)
    key_map = key_up.reshape(LATENT, head_count, NOPE_DIM)
    value_map = value_up.reshape(LATENT, head_count, VALUE_DIM)
    query_latent = jnp.einsum(
        "thn,lhn->thl", nope_heads, key_map, preferred_element_type=jnp.float32
    ).astype(jnp.bfloat16)
    grad_latent = jnp.einsum(
        "thv,lhv->thl", upstream, value_map, preferred_element_type=jnp.float32
    ).astype(jnp.bfloat16)
    row_delta = jnp.sum(grad_latent.astype(jnp.float32) * saved.astype(jnp.float32), axis=2)
    context_size = lax.axis_size(("inner", "outer"))
    my_index = lax.axis_index(("inner", "outer"))
    own_positions = key_positions(block_order, my_index * tokens, tokens, block_size)
    query_parts = []
    for target in range(2):
        offset = target * block_size
        positions = jnp.broadcast_to(
            own_positions[offset : offset + block_size, None], (block_size, head_count)
        ).reshape(flat_rows)
        lat_part = query_latent[offset : offset + block_size].reshape(flat_rows, LATENT)
        rope_part = rope_heads[offset : offset + block_size].reshape(flat_rows, ROPE_DIM)
        grad_part = grad_latent[offset : offset + block_size].reshape(flat_rows, LATENT)
        delta_part = row_delta[offset : offset + block_size].reshape(flat_rows)
        total_part = logsum[offset : offset + block_size].reshape(flat_rows)
        query_parts.append((lat_part, rope_part, positions, grad_part, delta_part, total_part))
    backward_pairs = tuple(query_parts)
    zero_grads = tuple(
        (
            (
                jnp.zeros((flat_rows, LATENT), jnp.float32),
                jnp.zeros((flat_rows, ROPE_DIM), jnp.float32),
            )
            for target in range(2)
        )
    )
    every_lat, every_rope = (
        lax.all_gather(latent, ("inner", "outer"), axis=0, tiled=True),
        lax.all_gather(key_rope, ("inner", "outer"), axis=0, tiled=True),
    )

    def visit_pair(query_grads, turn_index):
        lat_rows = []
        rope_rows = []
        for member in range(2):
            shard_index = 2 * turn_index + member
            lat_keys = lax.dynamic_slice_in_dim(every_lat, shard_index * tokens, tokens, 0)
            rope_keys = lax.dynamic_slice_in_dim(every_rope, shard_index * tokens, tokens, 0)
            positions = key_positions(block_order, shard_index * tokens, tokens, block_size)
            query_grads, contribution = shard_grads(
                backward_pairs, query_grads, lat_keys, rope_keys, positions
            )
            lat_rows.append(contribution[0])
            rope_rows.append(contribution[1])
        return (query_grads, (jnp.stack(lat_rows), jnp.stack(rope_rows)))

    query_grads, stacked = lax.scan(visit_pair, zero_grads, lax.iota(jnp.int32, context_size // 2))
    all_lat = stacked[0].reshape(context_size * tokens, LATENT)
    all_rope = stacked[1].reshape(context_size * tokens, ROPE_DIM)
    own_sums = sum_packed((all_lat, all_rope), ("inner", "outer"), (0, 0))
    summed = in_one((own_sums[0], own_sums[1]), "head")
    grad_query = jnp.concatenate([query_grads[0][0], query_grads[1][0]], axis=0)
    grad_query = grad_query.reshape(tokens, head_count, LATENT).astype(jnp.bfloat16)
    grad_rope = jnp.concatenate([query_grads[0][1], query_grads[1][1]], axis=0)
    d_query_rope = grad_rope.reshape(tokens, head_count * ROPE_DIM).astype(jnp.bfloat16)
    d_query_nope = jnp.einsum(
        "thl,lhn->thn", grad_query, key_map, preferred_element_type=jnp.float32
    )
    d_query_nope = d_query_nope.reshape(tokens, head_count * NOPE_DIM).astype(jnp.bfloat16)
    key_weight = jnp.einsum(
        "thl,thn->lhn", grad_query, nope_heads, preferred_element_type=jnp.float32
    )
    value_weight = jnp.einsum("thl,thv->lhv", saved, upstream, preferred_element_type=jnp.float32)
    weight_parts = side_by_side(
        (
            key_weight.reshape(LATENT, head_count * NOPE_DIM),
            value_weight.reshape(LATENT, head_count * VALUE_DIM),
        ),
        ("inner", "outer"),
        0,
        1,
    )
    return (
        d_query_nope,
        d_query_rope,
        summed[0].astype(jnp.bfloat16),
        summed[1].astype(jnp.bfloat16),
        weight_parts[0],
        weight_parts[1],
    )


def solution(mesh):
    placed = (
        P(("inner", "outer"), "head"),
        P(("inner", "outer"), "head"),
        P(("inner", "outer"), None),
        P(("inner", "outer"), None),
        P(None, "head"),
        P(None, "head"),
        P(("inner", "outer"), "head"),
        P(("inner", "outer"), "head"),
        P(("inner", "outer"), "head"),
        P(),
    )
    return jax.shard_map(
        local,
        mesh=mesh,
        in_specs=placed,
        out_specs=(
            P(("inner", "outer"), "head"),
            P(("inner", "outer"), "head"),
            P(("inner", "outer"), None),
            P(("inner", "outer"), None),
            P(("inner", "outer"), "head"),
            P(("inner", "outer"), "head"),
        ),
        check_vma=False,
    )
```

profile of v0, /device:TPU:12, one launch (start us, length us, event | category | flops | bytes accessed | tf_op | source)
XLA Modules:
  0.0 1754.9 jit_solution(2727139085759418729)
XLA Ops:
  26.4 42.6 %all_gather.7 = bf16[4096,64]{1,0:T(8,128)(2,1)} all-gather(bf16[128,64]{1,0:T(8,128)(2,1)S(1)} %copy.107), channel_id=1, replica_groups=mesh['head'=8,'inner'=2,'outer'=16] {'inner','outer'}, dimensions={0}, use_global_device_ids=true | all-gather | bytes 540672 | tf_op jit(solution)/shard_map/all_gather | solution.py:223
  82.8 1306.0 %while.24 = (s32[]{:T(128)}, f32[512,512]{1,0:T(8,128)S(1)}, f32[512,64]{0,1:T(8,128)}, f32[512,512]{1,0:T(8,128)}, f32[512,64]{0,1:T(8,128)}, /*index=5*/f32[16...) while((s32[]{:T(128)}, f32[512,512]{1,0:T(8,128)S(1)}, ...), condition=%wide.region_17.18_spmd.clone, body=%wide.region_2.17_spmd.clone.sunk | while | flops 1447517440 | bytes 55401404 | solution.py:241
  195.3 16.1 conditional.14
  264.7 16.1 conditional.14
  301.1 16.0 conditional.15
  350.7 16.1 conditional.14
  436.7 16.1 conditional.14
  473.1 16.0 conditional.15
  522.8 16.2 conditional.14
  559.3 16.0 conditional.15
  609.0 16.1 conditional.14
  695.0 16.1 conditional.14
  833.7 16.1 conditional.14
  919.6 16.1 conditional.14
  1005.4 16.1 conditional.14
  1041.8 16.0 conditional.15
  1111.4 16.0 conditional.15
  1161.0 16.1 conditional.14
  1197.4 16.0 conditional.15
  1247.1 16.2 conditional.14
  1283.6 16.0 conditional.15
  1333.3 16.1 conditional.14
  1433.6 184.8 %reduce-scatter.3.cloned.1.call-done = f32[576,128]{1,0:T(8,128)} async-done(((f32[18432,128]{1,0:T(8,128)}), f32[576,128]{1,0:T(8,128)}) %reduce-scatter.3.cloned.1.call-update) | async-done | bytes 294928 | tf_op jit(solution)/shard_map/reduce_scatter | solution.py:26
  1633.5 108.4 %reduce-scatter.5.cloned.1.call-done = f32[16,2048]{1,0:T(8,128)} async-done(((f32[512,2048]{1,0:T(8,128)}), f32[16,2048]{1,0:T(8,128)}) %reduce-scatter.5.cloned.1.call-update) | async-done | bytes 131088 | tf_op jit(solution)/shard_map/reduce_scatter | solution.py:59
  (1668 shorter events, 1791.6 us)
Async XLA Ops:
  7.2 10.8 copy-start
  7.2 72.5 %all-gather.2.cloned.1.call-start = ((), (), s32[]{:S(2)}) async-start(), calls=%async_computation.3 | async-start | bytes 4325376 | tf_op jit(solution)/shard_map/all_gather | solution.py:222
  7.9 1610.5 %reduce-scatter.3.cloned.1.call-start = ((), (), s32[]{:S(2)}) async-start(), calls=%async_computation.4 | async-start | bytes 9732096 | tf_op jit(solution)/shard_map/reduce_scatter | solution.py:26
  9.6 11.2 copy-start.36
  11.0 13.2 copy-start.45
  16.6 54.1 %copy-start.38 = (bf16[512,1024]{0,1:T(8,128)(2,1)}, bf16[512,1024]{0,1:T(8,128)(2,1)S(1)}, u32[]{:S(2)}) copy-start(bf16[512,1024]{0,1:T(8,128)(2,1)S(1)} %copy.139) | copy-start | bytes 3145732
  18.0 52.8 %copy-start.41 = (bf16[128,1024]{0,1:T(8,128)(2,1)}, bf16[128,1024]{0,1:T(8,128)(2,1)S(1)}, u32[]{:S(2)}) copy-start(bf16[128,1024]{0,1:T(8,128)(2,1)S(1)} %copy.140) | copy-start | bytes 786436
  129.1 16.6 copy-start.7
  284.5 16.6 copy-start.7
  370.5 16.6 copy-start.7
  456.6 16.6 copy-start.7
  542.8 16.6 copy-start.7
  628.8 16.6 copy-start.7
  767.7 16.5 copy-start.7
  853.6 16.5 copy-start.7
  939.4 16.5 copy-start.7
  1025.3 16.6 copy-start.7
  1094.8 16.6 copy-start.7
  1180.8 16.6 copy-start.7
  1267.0 16.6 copy-start.7
  1353.1 16.5 copy-start.7
  1419.9 322.0 %reduce-scatter.5.cloned.1.call-start = ((), (), s32[]{:S(2)}) async-start(), calls=%async_computation.5 | async-start | bytes 4325376 | tf_op jit(solution)/shard_map/reduce_scatter | solution.py:59
  1622.9 120.5 %all-to-all-start = ((f32[8,1,73728]{2,1,0:T(1,128)}), f32[8,1,73728]{2,1,0:T(1,128)}, u32[]{:S(2)}, u32[]{:S(2)}) async-start(f32[8,1,73728]{2,1,0:T(1,128)} %broadcast_in_dim.92), calls=%async_computation.1 | async-start | bytes 4718592 | tf_op jit(solution)/shard_map/all_to_all | solution.py:36
  1629.7 118.6 %copy-start.1 = (bf16[512,1024]{1,0:T(8,128)(2,1)S(1)}, bf16[512,1024]{1,0:T(8,128)(2,1)}, u32[]{:S(2)}) copy-start(bf16[512,1024]{1,0:T(8,128)(2,1)} %param.29) | copy-start | bytes 3145732
  (217 other events, 904.1 us)
Sparse Core Ops, SparseCore 0:
  9.9 69.7 all-gather.1
  1420.0 198.3 reduce-scatter.2
  1621.0 120.8 reduce-scatter.4
where the time goes:
time: 1790 us; the launch traced here: 1750 us
  matrix products  586 us (33%)
  local copies, waits for them, and re-layouts  517 us (29%)
  waiting for transfers between devices  302 us (17%)
  loops' own time  184 us (10%)
  other arithmetic  102 us (6%)
  blocking collectives  42.6 us (2%)
    dot_general x180, matrix products, contract_last(): lax.dot_general(first_op, second_op, (((1,), (1,)), ((), ())), preferred_...  281 us
    reduce_scatter x1, waiting for transfers between devices, sum_packed(): lax.psum_scatter(lines, axis, tiled=True).reshape(-1)  185 us
    another operation x1, loops' own time, local(): lax.scan(visit_pair, zero_grads, lax.iota(jnp.int32, context_size // 2))  179 us
    reduce_scatter x1, waiting for transfers between devices, side_by_side(): lax.psum_scatter(both, axis, scatter_dimension=dim, tiled=True)  108 us
    dot_general x60, matrix products, grad_update(): jnp.dot(rounded, queries[3], preferred_element_type=jnp.float32)  106 us
    dot_general x120, matrix products, contract_first(): lax.dot_general(first_op, second_op, (((0,), (0,)), ((), ())), preferred_...  92.3 us
    dynamic_update_slice x55, local copies, waits for them, and re-layouts, single_block(): lax.dynamic_update_slice_in_dim(carried[3], result[3], offset, 0)  78.1 us
    dot_general x60, matrix products, grad_update(): jnp.dot(dscore, queries[1], preferred_element_type=jnp.float32)  58.4 us
  transfers between devices with their start and end apart: 4, of which 3 were waited for; matrix products, arithmetic and copies ran while one was open for 2% of the time, Pallas kernels for 0%

commit v1 on v0

v1 whole, which is shorter than its diff:
```python
import jax
import jax.numpy as jnp
from jax import lax
from jax.experimental import pallas as pl
from jax.experimental.pallas import tpu as pltpu
from jax.sharding import Mesh, PartitionSpec as P

LATENT = 512
ROPE_DIM = 64
NOPE_DIM = 128
VALUE_DIM = 128
WIDE = 640
BLOCK = 64
HEADS_HERE = 8
FLAT = BLOCK * HEADS_HERE
TILE = 256
PER_TILE = TILE // BLOCK
FACTOR = float(NOPE_DIM + ROPE_DIM) ** -0.5

f32 = jnp.float32
bf16 = jnp.bfloat16


def dot_nt(a, b):
    return lax.dot_general(a, b, (((1,), (1,)), ((), ())), preferred_element_type=f32)


def dot_nn(a, b):
    return lax.dot_general(a, b, (((1,), (0,)), ((), ())), preferred_element_type=f32)


def dot_tn(a, b):
    return lax.dot_general(a, b, (((0,), (0,)), ((), ())), preferred_element_type=f32)


def split_parity(rows, count, core):
    pieces = rows.reshape(count, 2, rows.shape[0] // (2 * count), rows.shape[1])
    even = pieces[:, 0]
    odd = pieces[:, 1]
    return jnp.where(core == 0, even, odd), jnp.where(core == 0, odd, even)


def prepare_kernel(
    ids, nope, rope, key_up, value_up, saved, upstream, q_out, g_out, delta_out, keep, give
):
    core = ids[1]
    zeros = jnp.zeros((2 * BLOCK, WIDE - LATENT - ROPE_DIM), bf16)
    for h in range(HEADS_HERE):
        cols = slice(h * NOPE_DIM, (h + 1) * NOPE_DIM)
        wide = slice(h * LATENT, (h + 1) * LATENT)
        query = dot_nt(nope[:, cols], key_up[:, cols]).astype(bf16)
        grad = dot_nt(upstream[:, cols], value_up[:, cols]).astype(bf16)
        kept = saved[:, wide]
        delta_out[:, h : h + 1] = jnp.sum(
            grad.astype(f32) * kept.astype(f32), axis=1, keepdims=True
        )
        mine, other = split_parity(dot_tn(kept, upstream[:, cols]), keep.shape[0], core)
        keep[:, :, cols] = mine
        give[:, :, cols] = other.astype(bf16)
        tail = jnp.concatenate([rope[:, h * ROPE_DIM : (h + 1) * ROPE_DIM], zeros], axis=1)
        for j in range(2):
            rows = slice(j * BLOCK, (j + 1) * BLOCK)
            spot = slice(h * BLOCK, (h + 1) * BLOCK)
            q_out[j, spot, :LATENT] = query[rows]
            q_out[j, spot, LATENT:] = tail[rows]
            g_out[j, spot, :] = grad[rows]


def attend_kernel(
    order, ids, keys, q0, g0, v0, q1, g1, v1,
    dk_out, dq_own, dq_peer, where_at, place, seqs, dk_acc, acc_peer,
):
    core = ids[1]
    blocks = order.shape[0]
    chunk = dk_out.shape[1] * 2 * BLOCK // keys.shape[0]
    per_block = BLOCK // chunk

    def note(i, carry):
        where_at[order[i]] = i
        return carry

    lax.fori_loop(0, blocks, note, 0)
    shard = ids[0] * 2
    seq_of = [order[2 * (shard + side) + j] for side in (core, 1 - core) for j in range(2)]

    def pick(s, carry):
        at = where_at[s]
        here = ((at // 2) % 2 == core).astype(jnp.int32)
        place[carry[0]] = (at // 4) * 2 + at % 2
        seqs[carry[0]] = s
        counts = [n + here * (s <= own).astype(jnp.int32) for n, own in zip(carry[1:], seq_of)]
        return (carry[0] + here, *counts)

    counts = lax.fori_loop(0, blocks, pick, (jnp.int32(0),) * 5)[1:]
    dq_own[...] = jnp.zeros(dq_own.shape, f32)
    acc_peer[...] = jnp.zeros(acc_peer.shape, f32)
    key_at = lax.broadcasted_iota(jnp.int32, (BLOCK, FLAT), 0)
    query_at = lax.broadcasted_iota(jnp.int32, (TILE, FLAT), 1) % BLOCK

    def unit(tile, key_pos, qj, gj, vj, acc, j, own):
        scores = dot_nt(tile, qj[j]) * FACTOR
        dprobs = dot_nt(tile[:, :LATENT], gj[j])
        visible = key_pos <= query_at + own * BLOCK
        probs = jnp.exp(jnp.where(visible, scores - vj[j, 0:1, :], -1e30))
        dscore = (probs * (dprobs - vj[j, 1:2, :]) * FACTOR).astype(bf16)
        low_probs = probs.astype(bf16)
        acc[j] += dot_tn(dscore, tile)
        grad = dot_nn(dscore, qj[j])
        dk_acc[:, :LATENT] += grad[:, :LATENT] + dot_nn(low_probs, gj[j])
        dk_acc[:, LATENT:] += grad[:, LATENT:]

    def visit(t, carry):
        spots = [place[t * PER_TILE + i] for i in range(PER_TILE)]
        tile = jnp.concatenate([keys[pl.ds(k * BLOCK, BLOCK), :] for k in spots], axis=0)
        key_pos = jnp.concatenate(
            [key_at + seqs[t * PER_TILE + i] * BLOCK for i in range(PER_TILE)], axis=0
        )
        dk_acc[...] = jnp.zeros(dk_acc.shape, f32)
        sides = ((q0, g0, v0, dq_own), (q1, g1, v1, acc_peer))
        for n in range(4):
            @pl.when(t * PER_TILE < counts[n])
            def _():
                qj, gj, vj, acc = sides[n // 2]
                unit(tile, key_pos, qj, gj, vj, acc, n % 2, seq_of[n])
        for i, k in enumerate(spots):
            for piece in range(per_block):
                at = i * BLOCK + piece * chunk
                dk_out[(k % 2) * per_block + piece, pl.ds((k // 2) * chunk, chunk), :] = dk_acc[
                    at : at + chunk
                ].astype(bf16)
        return carry

    lax.fori_loop(0, keys.shape[0] // TILE, visit, 0)
    dq_peer[...] = acc_peer[...].astype(bf16)


def finish_kernel(ids, dq, dq_add, nope, key_up, dn_out, dr_out, keep, give):
    core = ids[1]
    for h in range(HEADS_HERE):
        cols = slice(h * NOPE_DIM, (h + 1) * NOPE_DIM)
        spot = slice(h * BLOCK, (h + 1) * BLOCK)
        both = [(dq[j, spot] + dq_add[j, spot].astype(f32)).astype(bf16) for j in range(2)]
        whole = jnp.concatenate(both, axis=0)
        grad = whole[:, :LATENT]
        dn_out[:, cols] = dot_nn(grad, key_up[:, cols]).astype(bf16)
        dr_out[:, h * ROPE_DIM : (h + 1) * ROPE_DIM] = whole[:, LATENT : LATENT + ROPE_DIM]
        mine, other = split_parity(dot_tn(grad, nope[:, cols]), keep.shape[0], core)
        keep[:, :, cols] = mine
        give[:, :, cols] = other.astype(bf16)


def in_vmem(count):
    return [pl.BlockSpec(memory_space=pltpu.VMEM)] * count


def in_smem(count):
    return [pl.BlockSpec(memory_space=pltpu.SMEM)] * count


def shape(dims, dtype):
    return jax.ShapeDtypeStruct(dims, dtype)


IZ = ("inner", "z")
GRP = ("inner", "z", "core")


def to_partner(x):
    return lax.ppermute(x, "core", [(0, 1), (1, 0)])


def exchange(x, axis):
    return lax.all_to_all(x, axis, split_axis=0, concat_axis=0, tiled=True)


def local(
    query_nope,
    query_rope,
    latent,
    key_rope,
    key_up,
    value_up,
    latent_out,
    out_grad,
    logsum,
    block_order,
):
    tokens = query_nope.shape[0]
    sets = lax.axis_size(IZ)
    heads = lax.axis_size("head")
    weight_rows = LATENT // (2 * sets)
    half = (sets, weight_rows, HEADS_HERE * NOPE_DIM)
    params = pltpu.CompilerParams(vmem_limit_bytes=58 * 1024 * 1024)
    ids = jnp.stack([lax.axis_index(IZ), lax.axis_index("core")]).astype(jnp.int32)
    mine = jnp.concatenate(
        [latent, key_rope, jnp.zeros((tokens, WIDE - LATENT - ROPE_DIM), bf16)], axis=1
    )
    keys = lax.all_gather(mine, IZ, axis=0, tiled=True)
    q, g, delta, value_keep, value_give = pl.pallas_call(
        prepare_kernel,
        in_specs=in_smem(1) + in_vmem(6),
        out_specs=in_vmem(5),
        out_shape=[
            shape((2, FLAT, WIDE), bf16),
            shape((2, FLAT, LATENT), bf16),
            shape((tokens, HEADS_HERE), f32),
            shape(half, f32),
            shape(half, bf16),
        ],
        compiler_params=params,
        name="prepare",
    )(ids, query_nope, query_rope, key_up, value_up, latent_out, out_grad)
    row_vals = jnp.stack([logsum, delta]).reshape(2, 2, BLOCK, HEADS_HERE)
    row_vals = row_vals.transpose(1, 0, 3, 2).reshape(2, 2, FLAT)
    q_peer, g_peer, vals_peer = to_partner(q), to_partner(g), to_partner(row_vals)
    value_part = (value_keep + to_partner(value_give).astype(f32)).astype(bf16)
    value_parts = exchange(value_part, IZ)
    value_parts, row_vals = lax.optimization_barrier((value_parts, row_vals))
    dk, dq, dq_give = pl.pallas_call(
        attend_kernel,
        in_specs=in_smem(2) + in_vmem(7),
        out_specs=in_vmem(3),
        out_shape=[
            shape((heads, sets * tokens // heads, WIDE), bf16),
            shape((2, FLAT, WIDE), f32),
            shape((2, FLAT, WIDE), bf16),
        ],
        scratch_shapes=[
            pltpu.SMEM((block_order.shape[0],), jnp.int32),
            pltpu.SMEM((block_order.shape[0],), jnp.int32),
            pltpu.SMEM((block_order.shape[0],), jnp.int32),
            pltpu.VMEM((TILE, WIDE), f32),
            pltpu.VMEM((2, FLAT, WIDE), f32),
        ],
        compiler_params=params,
        name="attend",
    )(block_order, ids, keys, q, g, row_vals, q_peer, g_peer, vals_peer)
    by_head = jnp.sum(exchange(dk, "head").astype(f32), axis=0).astype(bf16)
    dq_add = to_partner(dq_give)
    d_nope, d_rope, key_keep, key_give = pl.pallas_call(
        finish_kernel,
        in_specs=in_smem(1) + in_vmem(4),
        out_specs=in_vmem(4),
        out_shape=[
            shape(query_nope.shape, bf16),
            shape(query_rope.shape, bf16),
            shape(half, f32),
            shape(half, bf16),
        ],
        compiler_params=params,
        name="finish",
    )(ids, dq, dq_add, query_nope, key_up)
    by_set = exchange(by_head.reshape(sets, tokens // heads, WIDE), IZ)
    owned = jnp.sum(by_set.astype(f32), axis=0).astype(bf16)
    total = exchange(jnp.broadcast_to(owned, (heads, *owned.shape)), "head").reshape(tokens, WIDE)
    key_part = (key_keep + to_partner(key_give).astype(f32)).astype(bf16)
    key_grad = jnp.sum(exchange(key_part, IZ).astype(f32), axis=0)
    value_grad = jnp.sum(value_parts.astype(f32), axis=0)
    return (
        d_nope,
        d_rope,
        total[:, :LATENT],
        total[:, LATENT : LATENT + ROPE_DIM],
        key_grad,
        value_grad,
    )


def solution(mesh):
    heads, inner, outer = mesh.devices.shape
    fine = Mesh(
        mesh.devices.reshape(heads, inner, outer // 2, 2), ("head", "inner", "z", "core")
    )
    rows = P(GRP, "head")
    return jax.shard_map(
        local,
        mesh=fine,
        in_specs=(rows, rows, P(GRP, None), P(GRP, None), P(None, "head"), P(None, "head"),
                  rows, rows, rows, P()),
        out_specs=(rows, rows, P(GRP, None), P(GRP, None), rows, rows),
        check_vma=False,
    )
```

time: 1790 us -> 212 us (0.12); the launches traced: 1750 us -> 209 us
  matrix products: 586 us -> 0 us
  local copies, waits for them, and re-layouts: 517 us -> 4.28 us
  waiting for transfers between devices: 302 us -> 102 us
  loops' own time: 184 us -> 0 us
  other arithmetic: 102 us -> 9.33 us
  blocking collectives: 42.6 us -> 0 us
  Pallas kernels: 0 us -> 41.8 us
  starting transfers between devices: 6.96 us -> 37.5 us
    dot_general x485 -> x0, matrix products: 586 us -> none  [the longest x180 281 us: contract_last(): lax.dot_general(first_op, second_op, (((1,), (1,)), ((), ())), preferred_...]
    reduce_scatter x2 -> x0, waiting for transfers between devices: 293 us -> none  [the longest x1 185 us: sum_packed(): lax.psum_scatter(lines, axis, tiled=True).reshape(-1)]
    another operation x65 -> x0, loops' own time: 184 us -> none  [the longest x1 179 us: local(): lax.scan(visit_pair, zero_grads, lax.iota(jnp.int32, context_size // 2))]
    sub x120 -> x0, local copies, waits for them, and re-layouts: 102 us -> none  [the longest x60 50.9 us: grad_update(): scores - queries[5][None, :]]
    dynamic_slice x103 -> x0, local copies, waits for them, and re-layouts: 93.1 us -> none  [the longest x55 34.8 us: single_block(): part_pos = lax.dynamic_slice_in_dim(positions, offset, block_size, 0)]
    dynamic_update_slice x55 -> x0, local copies, waits for them, and re-layouts: 78.1 us -> none  [single_block(): lax.dynamic_update_slice_in_dim(carried[3], result[3], offset, 0)]
    slice x74 -> x2, local copies, waits for them, and re-layouts: 65.1 us -> 0.67 us  [the longest x1 0.66 us: local(): total[:, :LATENT]]
    all_to_all x1 -> x5, waiting for transfers between devices: 0.01 us -> 54.4 us  [exchange(): return lax.all_to_all(x, axis, split_axis=0, concat_axis=0, tiled=True)]
  transfers between devices with their start and end apart: 4 -> 12, of which waited for: 3 -> 8; matrix products, arithmetic and copies ran while one was open for 2% -> 4% of each run, Pallas kernels for 0% -> 5%
where the time goes in v1:
time: 212 us; the launch traced here: 209 us
  waiting for transfers between devices  102 us (48%)
  Pallas kernels  41.8 us (20%)
  starting transfers between devices  37.5 us (18%)
  between operations  14.2 us (7%)
  other arithmetic  9.33 us (4%)
  local copies, waits for them, and re-layouts  4.28 us (2%)
    all_to_all x5, waiting for transfers between devices, exchange(): return lax.all_to_all(x, axis, split_axis=0, concat_axis=0, tiled=True)  54.4 us
    all_gather x1, waiting for transfers between devices, local(): keys = lax.all_gather(mine, IZ, axis=0, tiled=True)  42.4 us
    all_to_all x5, starting transfers between devices, exchange(): return lax.all_to_all(x, axis, split_axis=0, concat_axis=0, tiled=True)  36.5 us
    pallas_call x1, Pallas kernels, local(): pl.pallas_call(attend_kernel, in_specs=in_smem(2) + in_vmem(7), out_specs...  32.2 us
    pallas_call x1, Pallas kernels, local(): pl.pallas_call(prepare_kernel, in_specs=in_smem(1) + in_vmem(6), out_spec...  5.1 us
    ppermute x6, waiting for transfers between devices, to_partner(): return lax.ppermute(x, 'core', [(0, 1), (1, 0)])  4.76 us
    pallas_call x1, Pallas kernels, local(): pl.pallas_call(finish_kernel, in_specs=in_smem(1) + in_vmem(4), out_specs...  4.51 us
  transfers between devices with their start and end apart: 12, of which 8 were waited for; matrix products, arithmetic and copies ran while one was open for 4% of the time, Pallas kernels for 5%

profile of v1, /device:TPU:12, one launch (start us, length us, event | category | flops | bytes accessed | tf_op | source)
XLA Modules:
  0.0 208.6 jit_solution(7541328227024519628)
XLA Ops:
  7.2 0.8 copy.24
  8.1 1.6 maximum_maximum_fusion
  10.4 5.1 %prepare.1 = (bf16[2,512,640]{2,1,0:T(8,128)(2,1)}, bf16[2,512,512]{2,1,0:T(8,128)(2,1)}, f32[128,8]{1,0:T(8,128)}, f32[16,16,1024]{2,1,0:T(8,128)}, bf16[16,16,1024]{2,1,0:T(8,128)(2,1)}) custom-call(s32[2]{0:T(128)} %pad_add_fusion.ids, bf16[128,1024]{1,0:T(8,128)(2,1)} %nope.3, bf16[128,512]{1,0:T(8,128)(2,1)} %rope.1, bf16[512,1024]{1,0:T(8,128)(2,1)} %key_up.3, ...), custom_call_target="tpu_custom_call" | custom-call | tf_op jit(solution)/shard_map/prepare/pallas_call | solution.py:199
  16.1 1.5 collective-permute-done
  17.7 2.2 %add_convert_fusion.1 = bf16[16,16,1024]{2,1,0:T(8,128)(2,1)} fusion(f32[16,16,1024]{2,1,0:T(8,128)} %get-tuple-element.22, bf16[16,16,1024]{2,1,0:T(8,128)(2,1)S(1)} %collective-permute-done), kind=kLoop, calls=%fused_computation.3 | loop fusion | flops 786432 | bytes 2097152 | tf_op jit(solution)/shard_map/convert_element_type | solution.py:216
  19.8 9.2 %all-to-all-start = ((bf16[16,16,1024]{2,1,0:T(8,128)(2,1)}), bf16[16,16,1024]{2,1,0:T(8,128)(2,1)S(1)}, u32[]{:S(2)}, u32[]{:S(2)}) async-start(bf16[16,16,1024]{2,1,0:T(8,128)(2,1)} %add_convert_fusion.1), calls=%async_computation | async-start | bytes 1048576 | tf_op jit(solution)/shard_map/all_to_all | solution.py:173
  29.4 20.1 %all-to-all-done = bf16[16,16,1024]{2,1,0:T(8,128)(2,1)S(1)} async-done(((bf16[16,16,1024]{2,1,0:T(8,128)(2,1)}), bf16[16,16,1024]{2,1,0:T(8,128)(2,1)S(1)}, u32[]{:S(2)}, u32[]{:S(2)}) %all-to-all-start) | async-done | bytes 524320 | tf_op jit(solution)/shard_map/all_to_all | solution.py:173
  49.6 42.4 %all-gather.2.cloned.1.call-done.keys = bf16[2048,640]{1,0:T(8,128)(2,1)} async-done(((bf16[128,640]{1,0:T(8,128)(2,1)}), bf16[2048,640]{1,0:T(8,128)(2,1)}) %all-gather.2.cloned.1.call-update) | async-done | bytes 2621456 | tf_op jit(solution)/shard_map/all_gather | solution.py:198
  91.9 32.2 %attend.1 = (bf16[8,256,640]{2,1,0:T(8,128)(2,1)}, f32[2,512,640]{2,1,0:T(8,128)}, bf16[2,512,640]{2,1,0:T(8,128)(2,1)}) custom-call(s32[64]{0:T(128)} %order.1, s32[2]{0:T(128)} %pad_add_fusion.ids, bf16[2048,640]{1,0:T(8,128)(2,1)} %all-gather.2.cloned.1.call-done.keys, bf16[2,512,640]{2,1,0:T(8,128)(2,1)} %get-tuple-element.20.q0, ...), custom_call_target="tpu_custom_call" | custom-call | tf_op jit(solution)/shard_map/attend/pallas_call | solution.py:219
  124.1 8.4 %all-to-all-start.1 = ((bf16[8,256,640]{2,1,0:T(8,128)(2,1)}), bf16[8,256,640]{2,1,0:T(8,128)(2,1)S(1)}, u32[]{:S(2)}, u32[]{:S(2)}) async-start(bf16[8,256,640]{2,1,0:T(8,128)(2,1)} %get-tuple-element.30), calls=%async_computation.1 | async-start | bytes 5242880 | tf_op jit(solution)/shard_map/all_to_all | solution.py:173
  132.5 3.2 %collective-permute-done.4.dq_add = bf16[2,512,640]{2,1,0:T(8,128)(2,1)S(1)} collective-permute-done((bf16[2,512,640]{2,1,0:T(8,128)(2,1)}, bf16[2,512,640]{2,1,0:T(8,128)(2,1)S(1)}, u32[]{:S(2)}, u32[]{:S(2)}) %collective-permute-start.4) | collective-permute-done | bytes 1310752 | tf_op jit(solution)/shard_map/ppermute | solution.py:169
  135.8 1.1 copy-done
  136.8 4.5 %finish.1 = (bf16[128,1024]{1,0:T(8,128)(2,1)}, bf16[128,512]{1,0:T(8,128)(2,1)}, f32[16,16,1024]{2,1,0:T(8,128)}, bf16[16,16,1024]{2,1,0:T(8,128)(2,1)}) custom-call(s32[2]{0:T(128)} %pad_add_fusion.ids, f32[2,512,640]{2,1,0:T(8,128)} %get-tuple-element.26.dq, bf16[2,512,640]{2,1,0:T(8,128)(2,1)} %copy-done, bf16[128,1024]{1,0:T(8,128)(2,1)} %nope.3, ...), custom_call_target="tpu_custom_call" | custom-call | tf_op jit(solution)/shard_map/finish/pallas_call | solution.py:240
  141.5 11.4 %all-to-all-done.1 = bf16[8,256,640]{2,1,0:T(8,128)(2,1)S(1)} async-done(((bf16[8,256,640]{2,1,0:T(8,128)(2,1)}), bf16[8,256,640]{2,1,0:T(8,128)(2,1)S(1)}, u32[]{:S(2)}, u32[]{:S(2)}) %all-to-all-start.1) | async-done | bytes 2621472 | tf_op jit(solution)/shard_map/all_to_all | solution.py:173
  152.9 1.2 reduce_sum.42
  154.1 4.0 %all-to-all-start.2 = ((bf16[16,16,640]{2,1,0:T(8,128)(2,1)}), bf16[16,16,640]{2,1,0:T(8,128)(2,1)S(1)}, u32[]{:S(2)}, u32[]{:S(2)}) async-start(bf16[16,16,640]{2,1,0:T(8,128)(2,1)} %bitcast.4), calls=%async_computation.2 | async-start | bytes 655360 | tf_op jit(solution)/shard_map/all_to_all | solution.py:173
  158.1 2.3 %add_convert_fusion = bf16[16,16,1024]{2,1,0:T(8,128)(2,1)} fusion(f32[16,16,1024]{2,1,0:T(8,128)} %get-tuple-element.31, bf16[16,16,1024]{2,1,0:T(8,128)(2,1)} %collective-permute-done.5), kind=kLoop, calls=%fused_computation.2 | loop fusion | flops 786432 | bytes 2097152 | tf_op jit(solution)/shard_map/convert_element_type | solution.py:256
  160.4 7.6 %all-to-all-done.2 = bf16[16,16,640]{2,1,0:T(8,128)(2,1)S(1)} async-done(((bf16[16,16,640]{2,1,0:T(8,128)(2,1)}), bf16[16,16,640]{2,1,0:T(8,128)(2,1)S(1)}, u32[]{:S(2)}, u32[]{:S(2)}) %all-to-all-start.2) | async-done | bytes 327712 | tf_op jit(solution)/shard_map/all_to_all | solution.py:173
  168.0 4.1 %all-to-all-start.4 = ((bf16[16,16,1024]{2,1,0:T(8,128)(2,1)}), bf16[16,16,1024]{2,1,0:T(8,128)(2,1)S(1)}, u32[]{:S(2)}, u32[]{:S(2)}) async-start(bf16[16,16,1024]{2,1,0:T(8,128)(2,1)} %add_convert_fusion), calls=%async_computation.4 | async-start | bytes 1048576 | tf_op jit(solution)/shard_map/all_to_all | solution.py:173
  172.1 12.1 %all-to-all-done.4 = bf16[16,16,1024]{2,1,0:T(8,128)(2,1)S(1)} async-done(((bf16[16,16,1024]{2,1,0:T(8,128)(2,1)}), bf16[16,16,1024]{2,1,0:T(8,128)(2,1)S(1)}, u32[]{:S(2)}, u32[]{:S(2)}) %all-to-all-start.4) | async-done | bytes 524320 | tf_op jit(solution)/shard_map/all_to_all | solution.py:173
  184.9 10.8 %all-to-all-start.3 = ((bf16[8,16,640]{2,1,0:T(8,128)(2,1)}), bf16[8,16,640]{2,1,0:T(8,128)(2,1)S(1)}, u32[]{:S(2)}, u32[]{:S(2)}) async-start(bf16[8,16,640]{2,1,0:T(8,128)(2,1)} %broadcast_in_dim.7), calls=%async_computation.3 | async-start | bytes 327680 | tf_op jit(solution)/shard_map/all_to_all | solution.py:173
  195.7 0.7 convert_reduce_fusion
  196.4 0.7 convert_reduce_fusion.1
  197.1 3.3 %all-to-all-done.3 = bf16[8,16,640]{2,1,0:T(8,128)(2,1)S(1)} async-done(((bf16[8,16,640]{2,1,0:T(8,128)(2,1)}), bf16[8,16,640]{2,1,0:T(8,128)(2,1)S(1)}, u32[]{:S(2)}, u32[]{:S(2)}) %all-to-all-start.3) | async-done | bytes 163872 | tf_op jit(solution)/shard_map/all_to_all | solution.py:173
  (38 shorter events, 4.0 us)
Async XLA Ops:
  7.2 84.8 %all-gather.2.cloned.1.call-start = ((), (), s32[]{:S(2)}) async-start(), calls=%async_computation.5 | async-start | bytes 2785280 | tf_op jit(solution)/shard_map/all_gather | solution.py:198
  10.4 18.7 %copy-start.6 = (f32[128,8]{0,1:T(8,128)S(1)}, f32[128,8]{0,1:T(8,128)}, u32[]{:S(2)}) copy-start(f32[128,8]{0,1:T(8,128)} %param.18) | copy-start | bytes 12292
  15.5 13.7 %copy-start.3 = (f32[128,8]{1,0:T(8,128)S(1)}, f32[128,8]{1,0:T(8,128)}, u32[]{:S(2)}) copy-start(f32[128,8]{1,0:T(8,128)} %get-tuple-element.24) | copy-start | bytes 12292
  15.5 2.2 %collective-permute-start = (bf16[16,16,1024]{2,1,0:T(8,128)(2,1)}, bf16[16,16,1024]{2,1,0:T(8,128)(2,1)S(1)}, u32[]{:S(2)}, u32[]{:S(2)}) collective-permute-start(bf16[16,16,1024]{2,1,0:T(8,128)(2,1)} %get-tuple-element.23), channel_id=1, source_target_pairs={{0,1},{1,0},{2,3},{3,2},{4,5},{5,4},{6,7},{7,6},{8,9},{9,8},{10,11... | collective-permute-start | bytes 1572872 | tf_op jit(solution)/shard_map/ppermute | solution.py:169
  15.6 34.0 %collective-permute-start.1 = (bf16[2,512,640]{2,1,0:T(8,128)(2,1)}, bf16[2,512,640]{2,1,0:T(8,128)(2,1)S(1)}, u32[]{:S(2)}, u32[]{:S(2)}) collective-permute-start(bf16[2,512,640]{2,1,0:T(8,128)(2,1)} %get-tuple-element.20.q0), channel_id=1, source_target_pairs={{0,1},{1,0},{2,3},{3,2},{4,5},{5,4},{6,7},{7,6},{8,9},{9,8},{10,11... | collective-permute-start | bytes 3932168 | tf_op jit(solution)/shard_map/ppermute | solution.py:169
  16.0 33.5 %collective-permute-start.2 = (bf16[2,512,512]{2,1,0:T(8,128)(2,1)}, bf16[2,512,512]{2,1,0:T(8,128)(2,1)S(1)}, u32[]{:S(2)}, u32[]{:S(2)}) collective-permute-start(bf16[2,512,512]{2,1,0:T(8,128)(2,1)} %get-tuple-element.21.g0), channel_id=1, source_target_pairs={{0,1},{1,0},{2,3},{3,2},{4,5},{5,4},{6,7},{7,6},{8,9},{9,8},{10,11... | collective-permute-start | bytes 3145736 | tf_op jit(solution)/shard_map/ppermute | solution.py:169
  19.8 29.7 %all-to-all-start = ((bf16[16,16,1024]{2,1,0:T(8,128)(2,1)}), bf16[16,16,1024]{2,1,0:T(8,128)(2,1)S(1)}, u32[]{:S(2)}, u32[]{:S(2)}) async-start(bf16[16,16,1024]{2,1,0:T(8,128)(2,1)} %add_convert_fusion.1), calls=%async_computation | async-start | bytes 1048576 | tf_op jit(solution)/shard_map/all_to_all | solution.py:173
  29.3 62.6 %copy-start.4 = (f32[2,2,512]{2,1,0:T(2,128)}, f32[2,2,512]{2,1,0:T(2,128)S(1)}, u32[]{:S(2)}) copy-start(f32[2,2,512]{2,1,0:T(2,128)S(1)} %reshape.26.v0) | copy-start | bytes 24580
  29.3 20.2 %collective-permute-start.3 = (f32[2,2,512]{2,1,0:T(2,128)S(1)}, f32[2,2,512]{2,1,0:T(2,128)S(1)}, u32[]{:S(2)}, u32[]{:S(2)}) collective-permute-start(f32[2,2,512]{2,1,0:T(2,128)S(1)} %reshape.26.v0), channel_id=1, source_target_pairs={{0,1},{1,0},{2,3},{3,2},{4,5},{5,4},{6,7},{7,6},{8,9},{9,8},{10,11... | collective-permute-start | bytes 24584 | tf_op jit(solution)/shard_map/ppermute | solution.py:169
  49.5 42.4 %copy-start.5 = (f32[2,2,512]{2,1,0:T(2,128)}, f32[2,2,512]{2,1,0:T(2,128)S(1)}, u32[]{:S(2)}) copy-start(f32[2,2,512]{2,1,0:T(2,128)S(1)} %collective-permute-done.3.v1) | copy-start | bytes 24580
  49.5 42.4 %copy-start.2 = (bf16[2,512,512]{2,1,0:T(8,128)(2,1)}, bf16[2,512,512]{2,1,0:T(8,128)(2,1)S(1)}, u32[]{:S(2)}) copy-start(bf16[2,512,512]{2,1,0:T(8,128)(2,1)S(1)} %collective-permute-done.2.g1) | copy-start | bytes 3145732
  49.6 42.4 %copy-start.1 = (bf16[2,512,640]{2,1,0:T(8,128)(2,1)}, bf16[2,512,640]{2,1,0:T(8,128)(2,1)S(1)}, u32[]{:S(2)}) copy-start(bf16[2,512,640]{2,1,0:T(8,128)(2,1)S(1)} %collective-permute-done.1.q1) | copy-start | bytes 3932164
  124.1 28.8 %all-to-all-start.1 = ((bf16[8,256,640]{2,1,0:T(8,128)(2,1)}), bf16[8,256,640]{2,1,0:T(8,128)(2,1)S(1)}, u32[]{:S(2)}, u32[]{:S(2)}) async-start(bf16[8,256,640]{2,1,0:T(8,128)(2,1)} %get-tuple-element.30), calls=%async_computation.1 | async-start | bytes 5242880 | tf_op jit(solution)/shard_map/all_to_all | solution.py:173
  132.5 3.2 %collective-permute-start.4 = (bf16[2,512,640]{2,1,0:T(8,128)(2,1)}, bf16[2,512,640]{2,1,0:T(8,128)(2,1)S(1)}, u32[]{:S(2)}, u32[]{:S(2)}) collective-permute-start(bf16[2,512,640]{2,1,0:T(8,128)(2,1)} %get-tuple-element.27), channel_id=1, source_target_pairs={{0,1},{1,0},{2,3},{3,2},{4,5},{5,4},{6,7},{7,6},{8,9},{9,8},{10,11... | collective-permute-start | bytes 3932168 | tf_op jit(solution)/shard_map/ppermute | solution.py:169
  135.8 1.1 copy-start
  141.4 16.8 %collective-permute-start.5 = (bf16[16,16,1024]{2,1,0:T(8,128)(2,1)}, bf16[16,16,1024]{2,1,0:T(8,128)(2,1)}, u32[]{:S(2)}, u32[]{:S(2)}) collective-permute-start(bf16[16,16,1024]{2,1,0:T(8,128)(2,1)} %get-tuple-element.32), channel_id=1, source_target_pairs={{0,1},{1,0},{2,3},{3,2},{4,5},{5,4},{6,7},{7,6},{8,9},{9,8},{10,11... | collective-permute-start | bytes 1572872 | tf_op jit(solution)/shard_map/ppermute | solution.py:169
  154.1 13.9 %all-to-all-start.2 = ((bf16[16,16,640]{2,1,0:T(8,128)(2,1)}), bf16[16,16,640]{2,1,0:T(8,128)(2,1)S(1)}, u32[]{:S(2)}, u32[]{:S(2)}) async-start(bf16[16,16,640]{2,1,0:T(8,128)(2,1)} %bitcast.4), calls=%async_computation.2 | async-start | bytes 655360 | tf_op jit(solution)/shard_map/all_to_all | solution.py:173
  168.0 16.2 %all-to-all-start.4 = ((bf16[16,16,1024]{2,1,0:T(8,128)(2,1)}), bf16[16,16,1024]{2,1,0:T(8,128)(2,1)S(1)}, u32[]{:S(2)}, u32[]{:S(2)}) async-start(bf16[16,16,1024]{2,1,0:T(8,128)(2,1)} %add_convert_fusion), calls=%async_computation.4 | async-start | bytes 1048576 | tf_op jit(solution)/shard_map/all_to_all | solution.py:173
  184.9 15.5 %all-to-all-start.3 = ((bf16[8,16,640]{2,1,0:T(8,128)(2,1)}), bf16[8,16,640]{2,1,0:T(8,128)(2,1)S(1)}, u32[]{:S(2)}, u32[]{:S(2)}) async-start(bf16[8,16,640]{2,1,0:T(8,128)(2,1)} %broadcast_in_dim.7), calls=%async_computation.3 | async-start | bytes 327680 | tf_op jit(solution)/shard_map/all_to_all | solution.py:173
Sparse Core Ops, SparseCore 0:
  10.3 81.5 all-gather.1

commit v2 on v1

--- a/solution.py
+++ b/solution.py
@@ -72,8 +72,8 @@
 ):
     core = ids[1]
     blocks = order.shape[0]
-    chunk = dk_out.shape[1] * 2 * BLOCK // keys.shape[0]
-    per_block = BLOCK // chunk
+    per_block = keys.shape[0] // 2
+    chunk = BLOCK // per_block
 
     def note(i, carry):
         where_at[order[i]] = i
@@ -111,7 +111,12 @@
 
     def visit(t, carry):
         spots = [place[t * PER_TILE + i] for i in range(PER_TILE)]
-        tile = jnp.concatenate([keys[pl.ds(k * BLOCK, BLOCK), :] for k in spots], axis=0)
+        pieces = [
+            ((k % 2) * per_block + piece, pl.ds((k // 2) * chunk, chunk))
+            for k in spots
+            for piece in range(per_block)
+        ]
+        tile = jnp.concatenate([keys[h, rows, :] for h, rows in pieces], axis=0)
         key_pos = jnp.concatenate(
             [key_at + seqs[t * PER_TILE + i] * BLOCK for i in range(PER_TILE)], axis=0
         )
@@ -122,15 +127,11 @@
             def _():
                 qj, gj, vj, acc = sides[n // 2]
                 unit(tile, key_pos, qj, gj, vj, acc, n % 2, seq_of[n])
-        for i, k in enumerate(spots):
-            for piece in range(per_block):
-                at = i * BLOCK + piece * chunk
-                dk_out[(k % 2) * per_block + piece, pl.ds((k // 2) * chunk, chunk), :] = dk_acc[
-                    at : at + chunk
-                ].astype(bf16)
+        for n, (h, rows) in enumerate(pieces):
+            dk_out[h, rows, :] = dk_acc[n * chunk : (n + 1) * chunk].astype(bf16)
         return carry
 
-    lax.fori_loop(0, keys.shape[0] // TILE, visit, 0)
+    lax.fori_loop(0, keys.shape[0] * keys.shape[1] // TILE, visit, 0)
     dq_peer[...] = acc_peer[...].astype(bf16)
 
 
@@ -171,6 +172,10 @@
 
 def exchange(x, axis):
     return lax.all_to_all(x, axis, split_axis=0, concat_axis=0, tiled=True)
+
+
+def to_all(x, axis):
+    return exchange(jnp.broadcast_to(x, (lax.axis_size(axis), *x.shape)), axis)
 
 
 def local(
@@ -192,10 +197,18 @@
     half = (sets, weight_rows, HEADS_HERE * NOPE_DIM)
     params = pltpu.CompilerParams(vmem_limit_bytes=58 * 1024 * 1024)
     ids = jnp.stack([lax.axis_index(IZ), lax.axis_index("core")]).astype(jnp.int32)
+    chunk = tokens // heads
+    first = lax.axis_index("head") * chunk
     mine = jnp.concatenate(
-        [latent, key_rope, jnp.zeros((tokens, WIDE - LATENT - ROPE_DIM), bf16)], axis=1
-    )
-    keys = lax.all_gather(mine, IZ, axis=0, tiled=True)
+        [
+            lax.dynamic_slice_in_dim(latent, first, chunk, 0),
+            lax.dynamic_slice_in_dim(key_rope, first, chunk, 0),
+            jnp.zeros((chunk, WIDE - LATENT - ROPE_DIM), bf16),
+        ],
+        axis=1,
+    )
+    slices = to_all(mine, IZ).reshape(sets * chunk, WIDE)
+    keys = to_all(slices, "head")
     q, g, delta, value_keep, value_give = pl.pallas_call(
         prepare_kernel,
         in_specs=in_smem(1) + in_vmem(6),
@@ -214,14 +227,14 @@
     row_vals = row_vals.transpose(1, 0, 3, 2).reshape(2, 2, FLAT)
     q_peer, g_peer, vals_peer = to_partner(q), to_partner(g), to_partner(row_vals)
     value_part = (value_keep + to_partner(value_give).astype(f32)).astype(bf16)
+    value_part, *_ = lax.optimization_barrier((value_part, keys, q_peer, g_peer, vals_peer))
     value_parts = exchange(value_part, IZ)
-    value_parts, row_vals = lax.optimization_barrier((value_parts, row_vals))
-    dk, dq, dq_give = pl.pallas_call(
+    attend = pl.pallas_call(
         attend_kernel,
         in_specs=in_smem(2) + in_vmem(7),
         out_specs=in_vmem(3),
         out_shape=[
-            shape((heads, sets * tokens // heads, WIDE), bf16),
+            shape((heads, sets * chunk, WIDE), bf16),
             shape((2, FLAT, WIDE), f32),
             shape((2, FLAT, WIDE), bf16),
         ],
@@ -234,7 +247,9 @@
         ],
         compiler_params=params,
         name="attend",
-    )(block_order, ids, keys, q, g, row_vals, q_peer, g_peer, vals_peer)
+    )
+    dk, dq, dq_give = attend(block_order, ids, keys, q, g, row_vals, q_peer, g_peer, vals_peer)
+    dk, value_parts = lax.optimization_barrier((dk, value_parts))
     by_head = jnp.sum(exchange(dk, "head").astype(f32), axis=0).astype(bf16)
     dq_add = to_partner(dq_give)
     d_nope, d_rope, key_keep, key_give = pl.pallas_call(
@@ -250,11 +265,12 @@
         compiler_params=params,
         name="finish",
     )(ids, dq, dq_add, query_nope, key_up)
-    by_set = exchange(by_head.reshape(sets, tokens // heads, WIDE), IZ)
-    owned = jnp.sum(by_set.astype(f32), axis=0).astype(bf16)
-    total = exchange(jnp.broadcast_to(owned, (heads, *owned.shape)), "head").reshape(tokens, WIDE)
     key_part = (key_keep + to_partner(key_give).astype(f32)).astype(bf16)
-    key_grad = jnp.sum(exchange(key_part, IZ).astype(f32), axis=0)
+    joined = jnp.concatenate([by_head.reshape(sets, chunk, WIDE), key_part], axis=2)
+    by_set = exchange(joined, IZ)
+    owned = jnp.sum(by_set[:, :, :WIDE].astype(f32), axis=0).astype(bf16)
+    key_grad = jnp.sum(by_set[:, :, WIDE:].astype(f32), axis=0)
+    total = to_all(owned, "head").reshape(tokens, WIDE)
     value_grad = jnp.sum(value_parts.astype(f32), axis=0)
     return (
         d_nope,

time: 212 us -> 186 us (0.88)
  waiting for transfers between devices: 102 us -> 67.5 us
  blocking collectives: 0 us -> 20.4 us
  between operations: 14.2 us -> 0.74 us
  local copies, waits for them, and re-layouts: 4.28 us -> 7.83 us
  starting transfers between devices: 37.5 us -> 35.1 us
    all_gather x1 -> x0, waiting for transfers between devices: 42.4 us -> none  [local(): keys = lax.all_gather(mine, IZ, axis=0, tiled=True)]
    all_to_all x0 -> x1, blocking collectives: none -> 20.4 us  [exchange(): return lax.all_to_all(x, axis, split_axis=0, concat_axis=0, tiled=True)]
    all_to_all x5, waiting for transfers between devices: 54.4 us -> 58.9 us  [exchange(): return lax.all_to_all(x, axis, split_axis=0, concat_axis=0, tiled=True)]
    ppermute x6, waiting for transfers between devices: 4.76 us -> 8.54 us  [to_partner(): return lax.ppermute(x, 'core', [(0, 1), (1, 0)])]
    all_to_all x5, starting transfers between devices: 36.5 us -> 33.9 us  [exchange(): return lax.all_to_all(x, axis, split_axis=0, concat_axis=0, tiled=True)]
  transfers between devices with their start and end apart: 12 -> 11, of which waited for: 8 -> 7; matrix products, arithmetic and copies ran while one was open for 4% -> 4% of each run, Pallas kernels for 5% -> 23%
where the time goes in v2:
time: 186 us; the launch traced here: 183 us
  waiting for transfers between devices  67.5 us (36%)
  Pallas kernels  41.7 us (22%)
  starting transfers between devices  35.1 us (19%)
  blocking collectives  20.4 us (11%)
  other arithmetic  9.67 us (5%)
  local copies, waits for them, and re-layouts  7.83 us (4%)
    all_to_all x5, waiting for transfers between devices, exchange(): return lax.all_to_all(x, axis, split_axis=0, concat_axis=0, tiled=True)  58.9 us
    all_to_all x5, starting transfers between devices, exchange(): return lax.all_to_all(x, axis, split_axis=0, concat_axis=0, tiled=True)  33.9 us
    pallas_call x1, Pallas kernels, local(): attend(block_order, ids, keys, q, g, row_vals, q_peer, g_peer, vals_peer)  32.1 us
    all_to_all x1, blocking collectives, exchange(): return lax.all_to_all(x, axis, split_axis=0, concat_axis=0, tiled=True)  20.4 us
    ppermute x6, waiting for transfers between devices, to_partner(): return lax.ppermute(x, 'core', [(0, 1), (1, 0)])  8.54 us
    pallas_call x1, Pallas kernels, local(): pl.pallas_call(prepare_kernel, in_specs=in_smem(1) + in_vmem(6), out_spec...  5.1 us
    pallas_call x1, Pallas kernels, local(): pl.pallas_call(finish_kernel, in_specs=in_smem(1) + in_vmem(4), out_specs...  4.46 us
  transfers between devices with their start and end apart: 11, of which 7 were waited for; matrix products, arithmetic and copies ran while one was open for 4% of the time, Pallas kernels for 23%

profile of v2, /device:TPU:12, one launch (start us, length us, event | category | flops | bytes accessed | tf_op | source)
XLA Modules:
  0.0 182.9 jit_solution(1693393985908462175)
XLA Ops:
  0.7 0.9 copy-done
  2.6 20.4 %all_to_all.30 = bf16[16,16,640]{2,1,0:T(8,128)(2,1)S(1)} all-to-all(bf16[16,16,640]{2,1,0:T(8,128)(2,1)S(1)} %broadcast_in_dim.13), channel_id=1, replica_groups=mesh['head'=8,'inner'=2,'z'=8,'core'=2] {'inner','z'}, dimensions={0} | all-to-all | bytes 655360 | tf_op jit(solution)/shard_map/all_to_all | solution.py:174
  23.0 1.7 broadcast_in_dim.14
  24.7 7.3 %all-to-all-start.1 = ((bf16[8,256,640]{2,1,0:T(8,128)(2,1)}), bf16[8,256,640]{2,1,0:T(8,128)(2,1)S(1)}, u32[]{:S(2)}, u32[]{:S(2)}) async-start(bf16[8,256,640]{2,1,0:T(8,128)(2,1)} %broadcast_in_dim.14), calls=%async_computation.1 | async-start | bytes 5242880 | tf_op jit(solution)/shard_map/all_to_all | solution.py:174
  32.6 5.1 %prepare.1 = (bf16[2,512,640]{2,1,0:T(8,128)(2,1)}, bf16[2,512,512]{2,1,0:T(8,128)(2,1)}, f32[128,8]{1,0:T(8,128)}, f32[16,16,1024]{2,1,0:T(8,128)}, bf16[16,16,1024]{2,1,0:T(8,128)(2,1)}) custom-call(s32[2]{0:T(128)} %pad_add_fusion.ids, bf16[128,1024]{1,0:T(8,128)(2,1)} %nope.3, bf16[128,512]{1,0:T(8,128)(2,1)} %rope.1, bf16[512,1024]{1,0:T(8,128)(2,1)} %key_up.3, ...), custom_call_target="tpu_custom_call" | custom-call | tf_op jit(solution)/shard_map/prepare/pallas_call | solution.py:212
  38.4 0.9 copy.22
  39.9 3.3 %collective-permute-done.4 = bf16[16,16,1024]{2,1,0:T(8,128)(2,1)S(1)} collective-permute-done((bf16[16,16,1024]{2,1,0:T(8,128)(2,1)}, bf16[16,16,1024]{2,1,0:T(8,128)(2,1)S(1)}, u32[]{:S(2)}, u32[]{:S(2)}) %collective-permute-start.4) | collective-permute-done | bytes 524320 | tf_op jit(solution)/shard_map/ppermute | solution.py:170
  43.2 2.2 %add_convert_fusion.1 = bf16[16,16,1024]{2,1,0:T(8,128)(2,1)} fusion(f32[16,16,1024]{2,1,0:T(8,128)} %get-tuple-element.29, bf16[16,16,1024]{2,1,0:T(8,128)(2,1)S(1)} %collective-permute-done.4), kind=kLoop, calls=%fused_computation.3 | loop fusion | flops 786432 | bytes 2097152 | tf_op jit(solution)/shard_map/convert_element_type | solution.py:229
  45.4 15.3 %all-to-all-done.1.keys = bf16[8,256,640]{2,1,0:T(8,128)(2,1)S(1)} async-done(((bf16[8,256,640]{2,1,0:T(8,128)(2,1)}), bf16[8,256,640]{2,1,0:T(8,128)(2,1)S(1)}, u32[]{:S(2)}, u32[]{:S(2)}) %all-to-all-start.1) | async-done | bytes 2621472 | tf_op jit(solution)/shard_map/all_to_all | solution.py:174
  60.7 6.1 %all-to-all-start.2 = ((bf16[16,16,1024]{2,1,0:T(8,128)(2,1)}), bf16[16,16,1024]{2,1,0:T(8,128)(2,1)S(1)}, u32[]{:S(2)}, u32[]{:S(2)}) async-start(bf16[16,16,1024]{2,1,0:T(8,128)(2,1)} %add_convert_fusion.1), calls=%async_computation.2 | async-start | bytes 1048576 | tf_op jit(solution)/shard_map/all_to_all | solution.py:174
  66.8 32.1 %attend.1 = (bf16[8,256,640]{2,1,0:T(8,128)(2,1)}, f32[2,512,640]{2,1,0:T(8,128)}, bf16[2,512,640]{2,1,0:T(8,128)(2,1)}) custom-call(s32[64]{0:T(128)} %order.1, s32[2]{0:T(128)} %pad_add_fusion.ids, bf16[8,256,640]{2,1,0:T(8,128)(2,1)} %copy-done.1, bf16[2,512,640]{2,1,0:T(8,128)(2,1)} %get-tuple-element.21.q0, bf16[2,512,512]{2,1,0:T(8,128)(2,1)} %get-tuple-element.22.g0, ...), custom_call_target="tpu_custom_call" | custom-call | tf_op jit(solution)/shard_map/attend/pallas_call | solution.py:251
  99.0 6.3 %all-to-all-start.3 = ((bf16[8,256,640]{2,1,0:T(8,128)(2,1)}), bf16[8,256,640]{2,1,0:T(8,128)(2,1)S(1)}, u32[]{:S(2)}, u32[]{:S(2)}) async-start(bf16[8,256,640]{2,1,0:T(8,128)(2,1)} %get-tuple-element.32), calls=%async_computation.3 | async-start | bytes 5242880 | tf_op jit(solution)/shard_map/all_to_all | solution.py:174
  105.3 3.2 %collective-permute-done.3.dq_add = bf16[2,512,640]{2,1,0:T(8,128)(2,1)S(1)} collective-permute-done((bf16[2,512,640]{2,1,0:T(8,128)(2,1)}, bf16[2,512,640]{2,1,0:T(8,128)(2,1)S(1)}, u32[]{:S(2)}, u32[]{:S(2)}) %collective-permute-start.3) | collective-permute-done | bytes 1310752 | tf_op jit(solution)/shard_map/ppermute | solution.py:170
  108.5 1.1 copy-done.2
  109.6 4.5 %finish.1 = (bf16[128,1024]{1,0:T(8,128)(2,1)}, bf16[128,512]{1,0:T(8,128)(2,1)}, f32[16,16,1024]{2,1,0:T(8,128)}, bf16[16,16,1024]{2,1,0:T(8,128)(2,1)}) custom-call(s32[2]{0:T(128)} %pad_add_fusion.ids, f32[2,512,640]{2,1,0:T(8,128)} %get-tuple-element.24.dq, bf16[2,512,640]{2,1,0:T(8,128)(2,1)} %copy-done.2, bf16[128,1024]{1,0:T(8,128)(2,1)} %nope.3, ...), custom_call_target="tpu_custom_call" | custom-call | tf_op jit(solution)/shard_map/finish/pallas_call | solution.py:255
  114.2 2.0 %collective-permute-done.5 = bf16[16,16,1024]{2,1,0:T(8,128)(2,1)S(1)} collective-permute-done((bf16[16,16,1024]{2,1,0:T(8,128)(2,1)}, bf16[16,16,1024]{2,1,0:T(8,128)(2,1)S(1)}, u32[]{:S(2)}, u32[]{:S(2)}) %collective-permute-start.5) | collective-permute-done | bytes 524320 | tf_op jit(solution)/shard_map/ppermute | solution.py:170
  116.2 2.2 %add_convert_fusion = bf16[16,16,1024]{2,1,0:T(8,128)(2,1)} fusion(f32[16,16,1024]{2,1,0:T(8,128)} %get-tuple-element.33, bf16[16,16,1024]{2,1,0:T(8,128)(2,1)S(1)} %collective-permute-done.5), kind=kLoop, calls=%fused_computation.2 | loop fusion | flops 786432 | bytes 2097152 | tf_op jit(solution)/shard_map/convert_element_type | solution.py:268
  118.4 17.3 %all-to-all-done.3 = bf16[8,256,640]{2,1,0:T(8,128)(2,1)S(1)} async-done(((bf16[8,256,640]{2,1,0:T(8,128)(2,1)}), bf16[8,256,640]{2,1,0:T(8,128)(2,1)S(1)}, u32[]{:S(2)}, u32[]{:S(2)}) %all-to-all-start.3) | async-done | bytes 2621472 | tf_op jit(solution)/shard_map/all_to_all | solution.py:174
  135.7 1.2 reduce_sum.42
  136.8 2.1 %pad_maximum_fusion = bf16[16,16,1664]{2,1,0:T(8,128)(2,1)} fusion(bf16[16,16,1024]{2,1,0:T(8,128)(2,1)} %add_convert_fusion, bf16[16,16,640]{2,1,0:T(8,128)(2,1)} %bitcast.12), kind=kLoop, calls=%fused_computation.4 | loop fusion | flops 1703936 | bytes 1703936 | tf_op jit(solution)/shard_map/concatenate | solution.py:269
  138.9 7.8 %all-to-all-start.4 = ((bf16[16,16,1664]{2,1,0:T(8,128)(2,1)}), bf16[16,16,1664]{2,1,0:T(8,128)(2,1)S(1)}, u32[]{:S(2)}, u32[]{:S(2)}) async-start(bf16[16,16,1664]{2,1,0:T(8,128)(2,1)} %pad_maximum_fusion), calls=%async_computation.4 | async-start | bytes 1703936 | tf_op jit(solution)/shard_map/all_to_all | solution.py:174
  147.5 22.4 %all-to-all-done.4 = bf16[16,16,1664]{2,1,0:T(8,128)(2,1)S(1)} async-done(((bf16[16,16,1664]{2,1,0:T(8,128)(2,1)}), bf16[16,16,1664]{2,1,0:T(8,128)(2,1)S(1)}, u32[]{:S(2)}, u32[]{:S(2)}) %all-to-all-start.4) | async-done | bytes 852000 | tf_op jit(solution)/shard_map/all_to_all | solution.py:174
  170.6 6.3 %all-to-all-start.5 = ((bf16[8,16,640]{2,1,0:T(8,128)(2,1)}), bf16[8,16,640]{2,1,0:T(8,128)(2,1)S(1)}, u32[]{:S(2)}, u32[]{:S(2)}) async-start(bf16[8,16,640]{2,1,0:T(8,128)(2,1)} %broadcast_in_dim.15), calls=%async_computation.5 | async-start | bytes 327680 | tf_op jit(solution)/shard_map/all_to_all | solution.py:174
  177.6 4.0 %all-to-all-done.5 = bf16[8,16,640]{2,1,0:T(8,128)(2,1)S(1)} async-done(((bf16[8,16,640]{2,1,0:T(8,128)(2,1)}), bf16[8,16,640]{2,1,0:T(8,128)(2,1)S(1)}, u32[]{:S(2)}, u32[]{:S(2)}) %all-to-all-start.5) | async-done | bytes 163872 | tf_op jit(solution)/shard_map/all_to_all | solution.py:174
  (39 shorter events, 6.5 us)
Async XLA Ops:
  0.6 0.9 copy-start
  24.7 36.0 %all-to-all-start.1 = ((bf16[8,256,640]{2,1,0:T(8,128)(2,1)}), bf16[8,256,640]{2,1,0:T(8,128)(2,1)S(1)}, u32[]{:S(2)}, u32[]{:S(2)}) async-start(bf16[8,256,640]{2,1,0:T(8,128)(2,1)} %broadcast_in_dim.14), calls=%async_computation.1 | async-start | bytes 5242880 | tf_op jit(solution)/shard_map/all_to_all | solution.py:174
  32.6 5.7 %copy-start.5 = (f32[128,8]{0,1:T(8,128)S(1)}, f32[128,8]{0,1:T(8,128)}, u32[]{:S(2)}) copy-start(f32[128,8]{0,1:T(8,128)} %param.18) | copy-start | bytes 12292
  37.7 7.7 %collective-permute-start = (bf16[2,512,640]{2,1,0:T(8,128)(2,1)}, bf16[2,512,640]{2,1,0:T(8,128)(2,1)}, u32[]{:S(2)}, u32[]{:S(2)}) collective-permute-start(bf16[2,512,640]{2,1,0:T(8,128)(2,1)} %get-tuple-element.21.q0), channel_id=1, source_target_pairs={{0,1},{1,0},{2,3},{3,2},{4,5},{5,4},{6,7},{7,6},{8,9},{9,8},{10,11... | collective-permute-start | bytes 3932168 | tf_op jit(solution)/shard_map/ppermute | solution.py:170
  37.7 7.7 %collective-permute-start.1 = (bf16[2,512,512]{2,1,0:T(8,128)(2,1)}, bf16[2,512,512]{2,1,0:T(8,128)(2,1)}, u32[]{:S(2)}, u32[]{:S(2)}) collective-permute-start(bf16[2,512,512]{2,1,0:T(8,128)(2,1)} %get-tuple-element.22.g0), channel_id=1, source_target_pairs={{0,1},{1,0},{2,3},{3,2},{4,5},{5,4},{6,7},{7,6},{8,9},{9,8},{10,11... | collective-permute-start | bytes 3145736 | tf_op jit(solution)/shard_map/ppermute | solution.py:170
  38.2 5.0 %collective-permute-start.4 = (bf16[16,16,1024]{2,1,0:T(8,128)(2,1)}, bf16[16,16,1024]{2,1,0:T(8,128)(2,1)S(1)}, u32[]{:S(2)}, u32[]{:S(2)}) collective-permute-start(bf16[16,16,1024]{2,1,0:T(8,128)(2,1)} %get-tuple-element.30), channel_id=1, source_target_pairs={{0,1},{1,0},{2,3},{3,2},{4,5},{5,4},{6,7},{7,6},{8,9},{9,8},{10,11... | collective-permute-start | bytes 1572872 | tf_op jit(solution)/shard_map/ppermute | solution.py:170
  39.4 27.4 %copy-start.3 = (f32[2,2,512]{2,1,0:T(2,128)}, f32[2,2,512]{2,1,0:T(2,128)S(1)}, u32[]{:S(2)}) copy-start(f32[2,2,512]{2,1,0:T(2,128)S(1)} %reshape.30.v0) | copy-start | bytes 24580
  39.4 6.0 %collective-permute-start.2 = (f32[2,2,512]{2,1,0:T(2,128)S(1)}, f32[2,2,512]{2,1,0:T(2,128)S(1)}, u32[]{:S(2)}, u32[]{:S(2)}) collective-permute-start(f32[2,2,512]{2,1,0:T(2,128)S(1)} %reshape.30.v0), channel_id=1, source_target_pairs={{0,1},{1,0},{2,3},{3,2},{4,5},{5,4},{6,7},{7,6},{8,9},{9,8},{10,11... | collective-permute-start | bytes 24584 | tf_op jit(solution)/shard_map/ppermute | solution.py:170
  45.4 21.5 %copy-start.4 = (f32[2,2,512]{2,1,0:T(2,128)}, f32[2,2,512]{2,1,0:T(2,128)S(1)}, u32[]{:S(2)}) copy-start(f32[2,2,512]{2,1,0:T(2,128)S(1)} %collective-permute-done.2.v1) | copy-start | bytes 24580
  60.7 6.2 %copy-start.1 = (bf16[8,256,640]{2,1,0:T(8,128)(2,1)}, bf16[8,256,640]{2,1,0:T(8,128)(2,1)S(1)}, u32[]{:S(2)}) copy-start(bf16[8,256,640]{2,1,0:T(8,128)(2,1)S(1)} %all-to-all-done.1.keys) | copy-start | bytes 7864324
  60.7 38.3 %all-to-all-start.2 = ((bf16[16,16,1024]{2,1,0:T(8,128)(2,1)}), bf16[16,16,1024]{2,1,0:T(8,128)(2,1)S(1)}, u32[]{:S(2)}, u32[]{:S(2)}) async-start(bf16[16,16,1024]{2,1,0:T(8,128)(2,1)} %add_convert_fusion.1), calls=%async_computation.2 | async-start | bytes 1048576 | tf_op jit(solution)/shard_map/all_to_all | solution.py:174
  99.0 36.7 %all-to-all-start.3 = ((bf16[8,256,640]{2,1,0:T(8,128)(2,1)}), bf16[8,256,640]{2,1,0:T(8,128)(2,1)S(1)}, u32[]{:S(2)}, u32[]{:S(2)}) async-start(bf16[8,256,640]{2,1,0:T(8,128)(2,1)} %get-tuple-element.32), calls=%async_computation.3 | async-start | bytes 5242880 | tf_op jit(solution)/shard_map/all_to_all | solution.py:174
  105.3 3.2 %collective-permute-start.3 = (bf16[2,512,640]{2,1,0:T(8,128)(2,1)}, bf16[2,512,640]{2,1,0:T(8,128)(2,1)S(1)}, u32[]{:S(2)}, u32[]{:S(2)}) collective-permute-start(bf16[2,512,640]{2,1,0:T(8,128)(2,1)} %get-tuple-element.25), channel_id=1, source_target_pairs={{0,1},{1,0},{2,3},{3,2},{4,5},{5,4},{6,7},{7,6},{8,9},{9,8},{10,11... | collective-permute-start | bytes 3932168 | tf_op jit(solution)/shard_map/ppermute | solution.py:170
  108.5 1.1 copy-start.2
  114.1 2.1 %collective-permute-start.5 = (bf16[16,16,1024]{2,1,0:T(8,128)(2,1)}, bf16[16,16,1024]{2,1,0:T(8,128)(2,1)S(1)}, u32[]{:S(2)}, u32[]{:S(2)}) collective-permute-start(bf16[16,16,1024]{2,1,0:T(8,128)(2,1)} %get-tuple-element.34), channel_id=1, source_target_pairs={{0,1},{1,0},{2,3},{3,2},{4,5},{5,4},{6,7},{7,6},{8,9},{9,8},{10,11... | collective-permute-start | bytes 1572872 | tf_op jit(solution)/shard_map/ppermute | solution.py:170
  138.9 30.9 %all-to-all-start.4 = ((bf16[16,16,1664]{2,1,0:T(8,128)(2,1)}), bf16[16,16,1664]{2,1,0:T(8,128)(2,1)S(1)}, u32[]{:S(2)}, u32[]{:S(2)}) async-start(bf16[16,16,1664]{2,1,0:T(8,128)(2,1)} %pad_maximum_fusion), calls=%async_computation.4 | async-start | bytes 1703936 | tf_op jit(solution)/shard_map/all_to_all | solution.py:174
  170.6 11.0 %all-to-all-start.5 = ((bf16[8,16,640]{2,1,0:T(8,128)(2,1)}), bf16[8,16,640]{2,1,0:T(8,128)(2,1)S(1)}, u32[]{:S(2)}, u32[]{:S(2)}) async-start(bf16[8,16,640]{2,1,0:T(8,128)(2,1)} %broadcast_in_dim.15), calls=%async_computation.5 | async-start | bytes 327680 | tf_op jit(solution)/shard_map/all_to_all | solution.py:174

commit v3 on v2

--- a/solution.py
+++ b/solution.py
@@ -8,7 +8,6 @@
 LATENT = 512
 ROPE_DIM = 64
 NOPE_DIM = 128
-VALUE_DIM = 128
 WIDE = 640
 BLOCK = 64
 HEADS_HERE = 8
@@ -68,7 +67,7 @@
 
 def attend_kernel(
     order, ids, keys, q0, g0, v0, q1, g1, v1,
-    dk_out, dq_own, dq_peer, where_at, place, seqs, dk_acc, acc_peer,
+    dk_out, dq_own, dq_peer, where_at, place, seqs, dk_acc, acc_own, acc_peer,
 ):
     core = ids[1]
     blocks = order.shape[0]
@@ -92,7 +91,7 @@
         return (carry[0] + here, *counts)
 
     counts = lax.fori_loop(0, blocks, pick, (jnp.int32(0),) * 5)[1:]
-    dq_own[...] = jnp.zeros(dq_own.shape, f32)
+    acc_own[...] = jnp.zeros(acc_own.shape, f32)
     acc_peer[...] = jnp.zeros(acc_peer.shape, f32)
     key_at = lax.broadcasted_iota(jnp.int32, (BLOCK, FLAT), 0)
     query_at = lax.broadcasted_iota(jnp.int32, (TILE, FLAT), 1) % BLOCK
@@ -121,7 +120,7 @@
             [key_at + seqs[t * PER_TILE + i] * BLOCK for i in range(PER_TILE)], axis=0
         )
         dk_acc[...] = jnp.zeros(dk_acc.shape, f32)
-        sides = ((q0, g0, v0, dq_own), (q1, g1, v1, acc_peer))
+        sides = ((q0, g0, v0, acc_own), (q1, g1, v1, acc_peer))
         for n in range(4):
             @pl.when(t * PER_TILE < counts[n])
             def _():
@@ -132,6 +131,7 @@
         return carry
 
     lax.fori_loop(0, keys.shape[0] * keys.shape[1] // TILE, visit, 0)
+    dq_own[...] = acc_own[...].astype(bf16)
     dq_peer[...] = acc_peer[...].astype(bf16)
 
 
@@ -140,7 +140,7 @@
     for h in range(HEADS_HERE):
         cols = slice(h * NOPE_DIM, (h + 1) * NOPE_DIM)
         spot = slice(h * BLOCK, (h + 1) * BLOCK)
-        both = [(dq[j, spot] + dq_add[j, spot].astype(f32)).astype(bf16) for j in range(2)]
+        both = [(dq[j, spot].astype(f32) + dq_add[j, spot].astype(f32)).astype(bf16) for j in range(2)]
         whole = jnp.concatenate(both, axis=0)
         grad = whole[:, :LATENT]
         dn_out[:, cols] = dot_nn(grad, key_up[:, cols]).astype(bf16)
@@ -178,7 +178,7 @@
     return exchange(jnp.broadcast_to(x, (lax.axis_size(axis), *x.shape)), axis)
 
 
-def local(
+def whole(
     query_nope,
     query_rope,
     latent,
@@ -208,8 +208,7 @@
         axis=1,
     )
     slices = to_all(mine, IZ).reshape(sets * chunk, WIDE)
-    keys = to_all(slices, "head")
-    q, g, delta, value_keep, value_give = pl.pallas_call(
+    prepare = pl.pallas_call(
         prepare_kernel,
         in_specs=in_smem(1) + in_vmem(6),
         out_specs=in_vmem(5),
@@ -222,12 +221,19 @@
         ],
         compiler_params=params,
         name="prepare",
-    )(ids, query_nope, query_rope, key_up, value_up, latent_out, out_grad)
+    )
+    q, g, delta, value_keep, value_give = prepare(
+        ids, query_nope, query_rope, key_up, value_up, latent_out, out_grad
+    )
     row_vals = jnp.stack([logsum, delta]).reshape(2, 2, BLOCK, HEADS_HERE)
     row_vals = row_vals.transpose(1, 0, 3, 2).reshape(2, 2, FLAT)
     q_peer, g_peer, vals_peer = to_partner(q), to_partner(g), to_partner(row_vals)
     value_part = (value_keep + to_partner(value_give).astype(f32)).astype(bf16)
-    value_part, *_ = lax.optimization_barrier((value_part, keys, q_peer, g_peer, vals_peer))
+    slices, value_part, q_peer, g_peer, vals_peer = lax.optimization_barrier(
+        (slices, value_part, q_peer, g_peer, vals_peer)
+    )
+    keys = to_all(slices, "head")
+    value_part, _ = lax.optimization_barrier((value_part, keys))
     value_parts = exchange(value_part, IZ)
     attend = pl.pallas_call(
         attend_kernel,
@@ -235,7 +241,7 @@
         out_specs=in_vmem(3),
         out_shape=[
             shape((heads, sets * chunk, WIDE), bf16),
-            shape((2, FLAT, WIDE), f32),
+            shape((2, FLAT, WIDE), bf16),
             shape((2, FLAT, WIDE), bf16),
         ],
         scratch_shapes=[
@@ -243,6 +249,7 @@
             pltpu.SMEM((block_order.shape[0],), jnp.int32),
             pltpu.SMEM((block_order.shape[0],), jnp.int32),
             pltpu.VMEM((TILE, WIDE), f32),
+            pltpu.VMEM((2, FLAT, WIDE), f32),
             pltpu.VMEM((2, FLAT, WIDE), f32),
         ],
         compiler_params=params,
@@ -289,7 +296,7 @@
     )
     rows = P(GRP, "head")
     return jax.shard_map(
-        local,
+        whole,
         mesh=fine,
         in_specs=(rows, rows, P(GRP, None), P(GRP, None), P(None, "head"), P(None, "head"),
                   rows, rows, rows, P()),

time: 186 us -> 190 us (1.022)
  blocking collectives: 20.4 us -> 36.5 us
  waiting for transfers between devices: 67.5 us -> 56.9 us
  starting transfers between devices: 35.1 us -> 39 us
  local copies, waits for them, and re-layouts: 7.83 us -> 5.43 us
  Pallas kernels: 41.7 us -> 39.7 us
    all_to_all x1, blocking collectives: 20.4 us -> 36.5 us  [exchange(): return lax.all_to_all(x, axis, split_axis=0, concat_axis=0, tiled=True)]
    all_to_all x5, waiting for transfers between devices: 58.9 us -> 51.6 us  [exchange(): return lax.all_to_all(x, axis, split_axis=0, concat_axis=0, tiled=True)]
    all_to_all x5, starting transfers between devices: 33.9 us -> 37.9 us  [exchange(): return lax.all_to_all(x, axis, split_axis=0, concat_axis=0, tiled=True)]
    ppermute x6, waiting for transfers between devices: 8.54 us -> 5.29 us  [to_partner(): return lax.ppermute(x, 'core', [(0, 1), (1, 0)])]
    pallas_call x3, Pallas kernels: 41.7 us -> 39.7 us  [the longest x1 30.5 us: whole(): attend(block_order, ids, keys, q, g, row_vals, q_peer, g_peer, vals_peer)]
  transfers between devices with their start and end apart: 11 -> 11, of which waited for: 7 -> 7; matrix products, arithmetic and copies ran while one was open for 4% -> 4% of each run, Pallas kernels for 23% -> 19%
where the time goes in v3:
time: 190 us; the launch traced here: 187 us
  waiting for transfers between devices  56.9 us (30%)
  Pallas kernels  39.7 us (21%)
  starting transfers between devices  39 us (21%)
  blocking collectives  36.5 us (19%)
  other arithmetic  8.49 us (4%)
  local copies, waits for them, and re-layouts  5.43 us (3%)
    all_to_all x5, waiting for transfers between devices, exchange(): return lax.all_to_all(x, axis, split_axis=0, concat_axis=0, tiled=True)  51.6 us
    all_to_all x5, starting transfers between devices, exchange(): return lax.all_to_all(x, axis, split_axis=0, concat_axis=0, tiled=True)  37.9 us
    all_to_all x1, blocking collectives, exchange(): return lax.all_to_all(x, axis, split_axis=0, concat_axis=0, tiled=True)  36.5 us
    pallas_call x1, Pallas kernels, whole(): attend(block_order, ids, keys, q, g, row_vals, q_peer, g_peer, vals_peer)  30.5 us
    ppermute x6, waiting for transfers between devices, to_partner(): return lax.ppermute(x, 'core', [(0, 1), (1, 0)])  5.29 us
    pallas_call x1, Pallas kernels, whole(): prepare(ids, query_nope, query_rope, key_up, value_up, latent_out, out_grad)  5.06 us
    pallas_call x1, Pallas kernels, whole(): pl.pallas_call(finish_kernel, in_specs=in_smem(1) + in_vmem(4), out_specs...  4.08 us
  transfers between devices with their start and end apart: 11, of which 7 were waited for; matrix products, arithmetic and copies ran while one was open for 4% of the time, Pallas kernels for 19%

profile of v3, /device:TPU:12, one launch (start us, length us, event | category | flops | bytes accessed | tf_op | source)
XLA Modules:
  0.0 186.6 jit_solution(10702671945684360652)
XLA Ops:
  1.2 5.1 %prepare.1 = (bf16[2,512,640]{2,1,0:T(8,128)(2,1)}, bf16[2,512,512]{2,1,0:T(8,128)(2,1)}, f32[128,8]{1,0:T(8,128)}, f32[16,16,1024]{2,1,0:T(8,128)}, bf16[16,16,1024]{2,1,0:T(8,128)(2,1)}) custom-call(s32[2]{0:T(128)} %pad_add_fusion.ids, bf16[128,1024]{1,0:T(8,128)(2,1)} %nope.3, bf16[128,512]{1,0:T(8,128)(2,1)} %rope.1, bf16[512,1024]{1,0:T(8,128)(2,1)} %key_up.3, ...), custom_call_target="tpu_custom_call" | custom-call | tf_op jit(solution)/shard_map/prepare/pallas_call | solution.py:225
  7.3 0.8 broadcast_in_dim.13
  8.1 9.2 %all-to-all-start = ((bf16[16,16,640]{2,1,0:T(8,128)(2,1)}), bf16[16,16,640]{2,1,0:T(8,128)(2,1)S(1)}, u32[]{:S(2)}, u32[]{:S(2)}) async-start(bf16[16,16,640]{2,1,0:T(8,128)(2,1)} %broadcast_in_dim.13), calls=%async_computation | async-start | bytes 655360 | tf_op jit(solution)/shard_map/all_to_all | solution.py:174
  17.4 0.9 copy.22
  18.6 1.0 add_convert_fusion.1
  19.6 9.4 %all-to-all-done = bf16[16,16,640]{2,1,0:T(8,128)(2,1)S(1)} async-done(((bf16[16,16,640]{2,1,0:T(8,128)(2,1)}), bf16[16,16,640]{2,1,0:T(8,128)(2,1)S(1)}, u32[]{:S(2)}, u32[]{:S(2)}) %all-to-all-start) | async-done | bytes 327712 | tf_op jit(solution)/shard_map/all_to_all | solution.py:174
  29.3 36.5 %all_to_all.30.keys = bf16[8,256,640]{2,1,0:T(8,128)(2,1)} all-to-all(bf16[8,256,640]{2,1,0:T(8,128)(2,1)S(1)} %broadcast_in_dim.14), channel_id=1, replica_groups=mesh['head'=8,'inner'=2,'z'=8,'core'=2] {'head'}, dimensions={0} | all-to-all | bytes 5242880 | tf_op jit(solution)/shard_map/all_to_all | solution.py:174
  65.7 5.9 %all-to-all-start.2 = ((bf16[16,16,1024]{2,1,0:T(8,128)(2,1)}), bf16[16,16,1024]{2,1,0:T(8,128)(2,1)S(1)}, u32[]{:S(2)}, u32[]{:S(2)}) async-start(bf16[16,16,1024]{2,1,0:T(8,128)(2,1)} %add_convert_fusion.1), calls=%async_computation.2 | async-start | bytes 1048576 | tf_op jit(solution)/shard_map/all_to_all | solution.py:174
  71.7 30.5 %attend.1 = (bf16[8,256,640]{2,1,0:T(8,128)(2,1)}, bf16[2,512,640]{2,1,0:T(8,128)(2,1)}, bf16[2,512,640]{2,1,0:T(8,128)(2,1)}) custom-call(s32[64]{0:T(128)} %order.1, s32[2]{0:T(128)} %pad_add_fusion.ids, bf16[8,256,640]{2,1,0:T(8,128)(2,1)} %all_to_all.30.keys, bf16[2,512,640]{2,1,0:T(8,128)(2,1)} %get-tuple-element.28.q0, ...), custom_call_target="tpu_custom_call" | custom-call | tf_op jit(solution)/shard_map/attend/pallas_call | solution.py:258
  102.2 6.8 %all-to-all-start.3 = ((bf16[8,256,640]{2,1,0:T(8,128)(2,1)}), bf16[8,256,640]{2,1,0:T(8,128)(2,1)S(1)}, u32[]{:S(2)}, u32[]{:S(2)}) async-start(bf16[8,256,640]{2,1,0:T(8,128)(2,1)} %get-tuple-element.42), calls=%async_computation.3 | async-start | bytes 5242880 | tf_op jit(solution)/shard_map/all_to_all | solution.py:174
  109.0 3.2 %collective-permute-done.4.dq_add = bf16[2,512,640]{2,1,0:T(8,128)(2,1)S(1)} collective-permute-done((bf16[2,512,640]{2,1,0:T(8,128)(2,1)}, bf16[2,512,640]{2,1,0:T(8,128)(2,1)S(1)}, u32[]{:S(2)}, u32[]{:S(2)}) %collective-permute-start.4) | collective-permute-done | bytes 1310752 | tf_op jit(solution)/shard_map/ppermute | solution.py:170
  112.2 1.1 copy-done.1
  113.3 4.1 %finish.1 = (bf16[128,1024]{1,0:T(8,128)(2,1)}, bf16[128,512]{1,0:T(8,128)(2,1)}, f32[16,16,1024]{2,1,0:T(8,128)}, bf16[16,16,1024]{2,1,0:T(8,128)(2,1)}) custom-call(s32[2]{0:T(128)} %pad_add_fusion.ids, bf16[2,512,640]{2,1,0:T(8,128)(2,1)} %get-tuple-element.35.dq, bf16[2,512,640]{2,1,0:T(8,128)(2,1)} %copy-done.1, bf16[128,1024]{1,0:T(8,128)(2,1)} %nope.3, ...), custom_call_target="tpu_custom_call" | custom-call | tf_op jit(solution)/shard_map/finish/pallas_call | solution.py:262
  117.5 2.0 %collective-permute-done.5 = bf16[16,16,1024]{2,1,0:T(8,128)(2,1)S(1)} collective-permute-done((bf16[16,16,1024]{2,1,0:T(8,128)(2,1)}, bf16[16,16,1024]{2,1,0:T(8,128)(2,1)S(1)}, u32[]{:S(2)}, u32[]{:S(2)}) %collective-permute-start.5) | collective-permute-done | bytes 524320 | tf_op jit(solution)/shard_map/ppermute | solution.py:170
  119.5 2.2 %add_convert_fusion = bf16[16,16,1024]{2,1,0:T(8,128)(2,1)} fusion(f32[16,16,1024]{2,1,0:T(8,128)} %get-tuple-element.43, bf16[16,16,1024]{2,1,0:T(8,128)(2,1)S(1)} %collective-permute-done.5), kind=kLoop, calls=%fused_computation.2 | loop fusion | flops 786432 | bytes 2097152 | tf_op jit(solution)/shard_map/convert_element_type | solution.py:275
  121.7 15.8 %all-to-all-done.3 = bf16[8,256,640]{2,1,0:T(8,128)(2,1)S(1)} async-done(((bf16[8,256,640]{2,1,0:T(8,128)(2,1)}), bf16[8,256,640]{2,1,0:T(8,128)(2,1)S(1)}, u32[]{:S(2)}, u32[]{:S(2)}) %all-to-all-start.3) | async-done | bytes 2621472 | tf_op jit(solution)/shard_map/all_to_all | solution.py:174
  137.5 1.2 reduce_sum.42
  138.7 2.1 %pad_maximum_fusion = bf16[16,16,1664]{2,1,0:T(8,128)(2,1)} fusion(bf16[16,16,1024]{2,1,0:T(8,128)(2,1)} %add_convert_fusion, bf16[16,16,640]{2,1,0:T(8,128)(2,1)} %bitcast.12), kind=kLoop, calls=%fused_computation.4 | loop fusion | flops 1703936 | bytes 1703936 | tf_op jit(solution)/shard_map/concatenate | solution.py:276
  140.8 9.7 %all-to-all-start.4 = ((bf16[16,16,1664]{2,1,0:T(8,128)(2,1)}), bf16[16,16,1664]{2,1,0:T(8,128)(2,1)S(1)}, u32[]{:S(2)}, u32[]{:S(2)}) async-start(bf16[16,16,1664]{2,1,0:T(8,128)(2,1)} %pad_maximum_fusion), calls=%async_computation.4 | async-start | bytes 1703936 | tf_op jit(solution)/shard_map/all_to_all | solution.py:174
  150.5 0.7 convert_reduce_fusion
  151.2 22.4 %all-to-all-done.4 = bf16[16,16,1664]{2,1,0:T(8,128)(2,1)S(1)} async-done(((bf16[16,16,1664]{2,1,0:T(8,128)(2,1)}), bf16[16,16,1664]{2,1,0:T(8,128)(2,1)S(1)}, u32[]{:S(2)}, u32[]{:S(2)}) %all-to-all-start.4) | async-done | bytes 852000 | tf_op jit(solution)/shard_map/all_to_all | solution.py:174
  174.3 6.3 %all-to-all-start.5 = ((bf16[8,16,640]{2,1,0:T(8,128)(2,1)}), bf16[8,16,640]{2,1,0:T(8,128)(2,1)S(1)}, u32[]{:S(2)}, u32[]{:S(2)}) async-start(bf16[8,16,640]{2,1,0:T(8,128)(2,1)} %broadcast_in_dim.15), calls=%async_computation.5 | async-start | bytes 327680 | tf_op jit(solution)/shard_map/all_to_all | solution.py:174
  180.6 0.7 convert_reduce_fusion.1
  181.3 4.0 %all-to-all-done.5 = bf16[8,16,640]{2,1,0:T(8,128)(2,1)S(1)} async-done(((bf16[8,16,640]{2,1,0:T(8,128)(2,1)}), bf16[8,16,640]{2,1,0:T(8,128)(2,1)S(1)}, u32[]{:S(2)}, u32[]{:S(2)}) %all-to-all-start.5) | async-done | bytes 163872 | tf_op jit(solution)/shard_map/all_to_all | solution.py:174
  (43 shorter events, 4.4 us)
Async XLA Ops:
  0.6 6.6 %copy-start = (bf16[128,512]{1,0:T(8,128)(2,1)S(1)}, bf16[128,512]{1,0:T(8,128)(2,1)}, u32[]{:S(2)}) copy-start(bf16[128,512]{1,0:T(8,128)(2,1)} %param.12) | copy-start | bytes 393220
  1.2 5.8 %copy-start.5 = (bf16[128,64]{0,1:T(8,128)(2,1)S(1)}, bf16[128,64]{0,1:T(8,128)(2,1)}, u32[]{:S(2)}) copy-start(bf16[128,64]{0,1:T(8,128)(2,1)} %param.13) | copy-start | bytes 49156
  1.2 16.0 %copy-start.7 = (f32[128,8]{0,1:T(8,128)S(1)}, f32[128,8]{0,1:T(8,128)}, u32[]{:S(2)}) copy-start(f32[128,8]{0,1:T(8,128)} %param.18) | copy-start | bytes 12292
  6.3 12.3 %copy-start.3 = (f32[16,16,1024]{2,1,0:T(8,128)S(1)}, f32[16,16,1024]{2,1,0:T(8,128)}, u32[]{:S(2)}) copy-start(f32[16,16,1024]{2,1,0:T(8,128)} %get-tuple-element.26) | copy-start | bytes 3145732
  6.3 22.7 %collective-permute-start.1 = (bf16[2,512,640]{2,1,0:T(8,128)(2,1)}, bf16[2,512,640]{2,1,0:T(8,128)(2,1)S(1)}, u32[]{:S(2)}, u32[]{:S(2)}) collective-permute-start(bf16[2,512,640]{2,1,0:T(8,128)(2,1)} %get-tuple-element.28.q0), channel_id=1, source_target_pairs={{0,1},{1,0},{2,3},{3,2},{4,5},{5,4},{6,7},{7,6},{8,9},{9,8},{10,11... | collective-permute-start | bytes 3932168 | tf_op jit(solution)/shard_map/ppermute | solution.py:170
  6.4 12.2 %collective-permute-start = (bf16[16,16,1024]{2,1,0:T(8,128)(2,1)}, bf16[16,16,1024]{2,1,0:T(8,128)(2,1)S(1)}, u32[]{:S(2)}, u32[]{:S(2)}) collective-permute-start(bf16[16,16,1024]{2,1,0:T(8,128)(2,1)} %get-tuple-element.27), channel_id=1, source_target_pairs={{0,1},{1,0},{2,3},{3,2},{4,5},{5,4},{6,7},{7,6},{8,9},{9,8},{10,11... | collective-permute-start | bytes 1572872 | tf_op jit(solution)/shard_map/ppermute | solution.py:170
  6.9 22.1 %collective-permute-start.2 = (bf16[2,512,512]{2,1,0:T(8,128)(2,1)}, bf16[2,512,512]{2,1,0:T(8,128)(2,1)}, u32[]{:S(2)}, u32[]{:S(2)}) collective-permute-start(bf16[2,512,512]{2,1,0:T(8,128)(2,1)} %get-tuple-element.29.g0), channel_id=1, source_target_pairs={{0,1},{1,0},{2,3},{3,2},{4,5},{5,4},{6,7},{7,6},{8,9},{9,8},{10,11... | collective-permute-start | bytes 3145736 | tf_op jit(solution)/shard_map/ppermute | solution.py:170
  8.1 21.0 %all-to-all-start = ((bf16[16,16,640]{2,1,0:T(8,128)(2,1)}), bf16[16,16,640]{2,1,0:T(8,128)(2,1)S(1)}, u32[]{:S(2)}, u32[]{:S(2)}) async-start(bf16[16,16,640]{2,1,0:T(8,128)(2,1)} %broadcast_in_dim.13), calls=%async_computation | async-start | bytes 655360 | tf_op jit(solution)/shard_map/all_to_all | solution.py:174
  18.4 10.9 %copy-start.4 = (f32[2,2,512]{2,1,0:T(2,128)}, f32[2,2,512]{2,1,0:T(2,128)S(1)}, u32[]{:S(2)}) copy-start(f32[2,2,512]{2,1,0:T(2,128)S(1)} %reshape.30.v0) | copy-start | bytes 24580
  18.4 1.3 collective-permute-start.3
  19.6 46.1 %copy-start.6 = (f32[2,2,512]{2,1,0:T(2,128)}, f32[2,2,512]{2,1,0:T(2,128)S(1)}, u32[]{:S(2)}) copy-start(f32[2,2,512]{2,1,0:T(2,128)S(1)} %collective-permute-done.3.v1) | copy-start | bytes 24580
  29.0 36.7 %copy-start.2 = (bf16[2,512,640]{2,1,0:T(8,128)(2,1)}, bf16[2,512,640]{2,1,0:T(8,128)(2,1)S(1)}, u32[]{:S(2)}) copy-start(bf16[2,512,640]{2,1,0:T(8,128)(2,1)S(1)} %collective-permute-done.1.q1) | copy-start | bytes 3932164
  65.7 36.4 %all-to-all-start.2 = ((bf16[16,16,1024]{2,1,0:T(8,128)(2,1)}), bf16[16,16,1024]{2,1,0:T(8,128)(2,1)S(1)}, u32[]{:S(2)}, u32[]{:S(2)}) async-start(bf16[16,16,1024]{2,1,0:T(8,128)(2,1)} %add_convert_fusion.1), calls=%async_computation.2 | async-start | bytes 1048576 | tf_op jit(solution)/shard_map/all_to_all | solution.py:174
  102.2 35.3 %all-to-all-start.3 = ((bf16[8,256,640]{2,1,0:T(8,128)(2,1)}), bf16[8,256,640]{2,1,0:T(8,128)(2,1)S(1)}, u32[]{:S(2)}, u32[]{:S(2)}) async-start(bf16[8,256,640]{2,1,0:T(8,128)(2,1)} %get-tuple-element.42), calls=%async_computation.3 | async-start | bytes 5242880 | tf_op jit(solution)/shard_map/all_to_all | solution.py:174
  109.0 3.2 %collective-permute-start.4 = (bf16[2,512,640]{2,1,0:T(8,128)(2,1)}, bf16[2,512,640]{2,1,0:T(8,128)(2,1)S(1)}, u32[]{:S(2)}, u32[]{:S(2)}) collective-permute-start(bf16[2,512,640]{2,1,0:T(8,128)(2,1)} %get-tuple-element.36), channel_id=1, source_target_pairs={{0,1},{1,0},{2,3},{3,2},{4,5},{5,4},{6,7},{7,6},{8,9},{9,8},{10,11... | collective-permute-start | bytes 3932168 | tf_op jit(solution)/shard_map/ppermute | solution.py:170
  112.2 1.1 copy-start.1
  117.4 2.1 %collective-permute-start.5 = (bf16[16,16,1024]{2,1,0:T(8,128)(2,1)}, bf16[16,16,1024]{2,1,0:T(8,128)(2,1)S(1)}, u32[]{:S(2)}, u32[]{:S(2)}) collective-permute-start(bf16[16,16,1024]{2,1,0:T(8,128)(2,1)} %get-tuple-element.44), channel_id=1, source_target_pairs={{0,1},{1,0},{2,3},{3,2},{4,5},{5,4},{6,7},{7,6},{8,9},{9,8},{10,11... | collective-permute-start | bytes 1572872 | tf_op jit(solution)/shard_map/ppermute | solution.py:170
  140.8 32.8 %all-to-all-start.4 = ((bf16[16,16,1664]{2,1,0:T(8,128)(2,1)}), bf16[16,16,1664]{2,1,0:T(8,128)(2,1)S(1)}, u32[]{:S(2)}, u32[]{:S(2)}) async-start(bf16[16,16,1664]{2,1,0:T(8,128)(2,1)} %pad_maximum_fusion), calls=%async_computation.4 | async-start | bytes 1703936 | tf_op jit(solution)/shard_map/all_to_all | solution.py:174
  174.3 11.0 %all-to-all-start.5 = ((bf16[8,16,640]{2,1,0:T(8,128)(2,1)}), bf16[8,16,640]{2,1,0:T(8,128)(2,1)S(1)}, u32[]{:S(2)}, u32[]{:S(2)}) async-start(bf16[8,16,640]{2,1,0:T(8,128)(2,1)} %broadcast_in_dim.15), calls=%async_computation.5 | async-start | bytes 327680 | tf_op jit(solution)/shard_map/all_to_all | solution.py:174

commit v4 on v2

--- a/solution.py
+++ b/solution.py
@@ -13,7 +13,9 @@
 BLOCK = 64
 HEADS_HERE = 8
 FLAT = BLOCK * HEADS_HERE
-TILE = 256
+TILE = 512
+LANES = 128
+SLABS = LATENT // LANES
 PER_TILE = TILE // BLOCK
 FACTOR = float(NOPE_DIM + ROPE_DIM) ** -0.5
 
@@ -55,8 +57,9 @@
             grad.astype(f32) * kept.astype(f32), axis=1, keepdims=True
         )
         mine, other = split_parity(dot_tn(kept, upstream[:, cols]), keep.shape[0], core)
-        keep[:, :, cols] = mine
-        give[:, :, cols] = other.astype(bf16)
+        slab = slice(h * mine.shape[1], (h + 1) * mine.shape[1])
+        keep[:, slab, :] = mine
+        give[:, slab, :] = other.astype(bf16)
         tail = jnp.concatenate([rope[:, h * ROPE_DIM : (h + 1) * ROPE_DIM], zeros], axis=1)
         for j in range(2):
             rows = slice(j * BLOCK, (j + 1) * BLOCK)
@@ -68,7 +71,7 @@
 
 def attend_kernel(
     order, ids, keys, q0, g0, v0, q1, g1, v1,
-    dk_out, dq_own, dq_peer, where_at, place, seqs, dk_acc, acc_peer,
+    dk_out, dq_own, dq_peer, where_at, place, seqs, dk_acc, acc_own, acc_peer,
 ):
     core = ids[1]
     blocks = order.shape[0]
@@ -92,7 +95,7 @@
         return (carry[0] + here, *counts)
 
     counts = lax.fori_loop(0, blocks, pick, (jnp.int32(0),) * 5)[1:]
-    dq_own[...] = jnp.zeros(dq_own.shape, f32)
+    acc_own[...] = jnp.zeros(acc_own.shape, f32)
     acc_peer[...] = jnp.zeros(acc_peer.shape, f32)
     key_at = lax.broadcasted_iota(jnp.int32, (BLOCK, FLAT), 0)
     query_at = lax.broadcasted_iota(jnp.int32, (TILE, FLAT), 1) % BLOCK
@@ -109,29 +112,42 @@
         dk_acc[:, :LATENT] += grad[:, :LATENT] + dot_nn(low_probs, gj[j])
         dk_acc[:, LATENT:] += grad[:, LATENT:]
 
+    def unpack(h, s):
+        slabs = [keys[h, s, i * chunk : (i + 1) * chunk, :] for i in range(SLABS)]
+        rot = keys[h, s, SLABS * chunk :, :].astype(f32)
+        both = jnp.concatenate([rot, pltpu.roll(rot, ROPE_DIM, 1)], axis=0).astype(bf16)
+        return jnp.concatenate([*slabs, both], axis=1)
+
     def visit(t, carry):
         spots = [place[t * PER_TILE + i] for i in range(PER_TILE)]
         pieces = [
-            ((k % 2) * per_block + piece, pl.ds((k // 2) * chunk, chunk))
-            for k in spots
-            for piece in range(per_block)
+            ((k % 2) * per_block + piece, k // 2) for k in spots for piece in range(per_block)
         ]
-        tile = jnp.concatenate([keys[h, rows, :] for h, rows in pieces], axis=0)
+        tile = jnp.concatenate([unpack(h, s) for h, s in pieces], axis=0)
         key_pos = jnp.concatenate(
             [key_at + seqs[t * PER_TILE + i] * BLOCK for i in range(PER_TILE)], axis=0
         )
         dk_acc[...] = jnp.zeros(dk_acc.shape, f32)
-        sides = ((q0, g0, v0, dq_own), (q1, g1, v1, acc_peer))
+        sides = ((q0, g0, v0, acc_own), (q1, g1, v1, acc_peer))
         for n in range(4):
             @pl.when(t * PER_TILE < counts[n])
             def _():
                 qj, gj, vj, acc = sides[n // 2]
                 unit(tile, key_pos, qj, gj, vj, acc, n % 2, seq_of[n])
-        for n, (h, rows) in enumerate(pieces):
-            dk_out[h, rows, :] = dk_acc[n * chunk : (n + 1) * chunk].astype(bf16)
+        for n, (h, s) in enumerate(pieces):
+            part = dk_acc[n * chunk : (n + 1) * chunk]
+            for i in range(SLABS):
+                dk_out[h, s, i * chunk : (i + 1) * chunk, :] = part[
+                    :, i * LANES : (i + 1) * LANES
+                ].astype(bf16)
+            rot = part[:, LATENT:]
+            dk_out[h, s, SLABS * chunk :, :] = (
+                rot[: chunk // 2] + pltpu.roll(rot[chunk // 2 :], ROPE_DIM, 1)
+            ).astype(bf16)
         return carry
 
-    lax.fori_loop(0, keys.shape[0] * keys.shape[1] // TILE, visit, 0)
+    lax.fori_loop(0, keys.shape[1] * 2 * BLOCK // TILE, visit, 0)
+    dq_own[...] = acc_own[...].astype(bf16)
     dq_peer[...] = acc_peer[...].astype(bf16)
 
 
@@ -140,14 +156,15 @@
     for h in range(HEADS_HERE):
         cols = slice(h * NOPE_DIM, (h + 1) * NOPE_DIM)
         spot = slice(h * BLOCK, (h + 1) * BLOCK)
-        both = [(dq[j, spot] + dq_add[j, spot].astype(f32)).astype(bf16) for j in range(2)]
+        both = [(dq[j, spot].astype(f32) + dq_add[j, spot].astype(f32)).astype(bf16) for j in range(2)]
         whole = jnp.concatenate(both, axis=0)
         grad = whole[:, :LATENT]
         dn_out[:, cols] = dot_nn(grad, key_up[:, cols]).astype(bf16)
         dr_out[:, h * ROPE_DIM : (h + 1) * ROPE_DIM] = whole[:, LATENT : LATENT + ROPE_DIM]
         mine, other = split_parity(dot_tn(grad, nope[:, cols]), keep.shape[0], core)
-        keep[:, :, cols] = mine
-        give[:, :, cols] = other.astype(bf16)
+        slab = slice(h * mine.shape[1], (h + 1) * mine.shape[1])
+        keep[:, slab, :] = mine
+        give[:, slab, :] = other.astype(bf16)
 
 
 def in_vmem(count):
@@ -194,21 +211,18 @@
     sets = lax.axis_size(IZ)
     heads = lax.axis_size("head")
     weight_rows = LATENT // (2 * sets)
-    half = (sets, weight_rows, HEADS_HERE * NOPE_DIM)
+    half = (sets, HEADS_HERE * weight_rows, LANES)
     params = pltpu.CompilerParams(vmem_limit_bytes=58 * 1024 * 1024)
     ids = jnp.stack([lax.axis_index(IZ), lax.axis_index("core")]).astype(jnp.int32)
     chunk = tokens // heads
     first = lax.axis_index("head") * chunk
-    mine = jnp.concatenate(
-        [
-            lax.dynamic_slice_in_dim(latent, first, chunk, 0),
-            lax.dynamic_slice_in_dim(key_rope, first, chunk, 0),
-            jnp.zeros((chunk, WIDE - LATENT - ROPE_DIM), bf16),
-        ],
-        axis=1,
-    )
-    slices = to_all(mine, IZ).reshape(sets * chunk, WIDE)
-    keys = to_all(slices, "head")
+    lat = lax.dynamic_slice_in_dim(latent, first, chunk, 0)
+    rot = lax.dynamic_slice_in_dim(key_rope, first, chunk, 0)
+    slabs = [lat[:, i * LANES : (i + 1) * LANES] for i in range(SLABS)]
+    paired = jnp.concatenate([rot[: chunk // 2], rot[chunk // 2 :]], axis=1)
+    mine = jnp.concatenate([*slabs, paired], axis=0)
+    packed = mine.shape[0]
+    keys = to_all(to_all(mine, IZ), "head")
     q, g, delta, value_keep, value_give = pl.pallas_call(
         prepare_kernel,
         in_specs=in_smem(1) + in_vmem(6),
@@ -234,8 +248,8 @@
         in_specs=in_smem(2) + in_vmem(7),
         out_specs=in_vmem(3),
         out_shape=[
-            shape((heads, sets * chunk, WIDE), bf16),
-            shape((2, FLAT, WIDE), f32),
+            shape((heads, sets, packed, LANES), bf16),
+            shape((2, FLAT, WIDE), bf16),
             shape((2, FLAT, WIDE), bf16),
         ],
         scratch_shapes=[
@@ -243,6 +257,7 @@
             pltpu.SMEM((block_order.shape[0],), jnp.int32),
             pltpu.SMEM((block_order.shape[0],), jnp.int32),
             pltpu.VMEM((TILE, WIDE), f32),
+            pltpu.VMEM((2, FLAT, WIDE), f32),
             pltpu.VMEM((2, FLAT, WIDE), f32),
         ],
         compiler_params=params,
@@ -266,19 +281,26 @@
         name="finish",
     )(ids, dq, dq_add, query_nope, key_up)
     key_part = (key_keep + to_partner(key_give).astype(f32)).astype(bf16)
-    joined = jnp.concatenate([by_head.reshape(sets, chunk, WIDE), key_part], axis=2)
-    by_set = exchange(joined, IZ)
-    owned = jnp.sum(by_set[:, :, :WIDE].astype(f32), axis=0).astype(bf16)
-    key_grad = jnp.sum(by_set[:, :, WIDE:].astype(f32), axis=0)
-    total = to_all(owned, "head").reshape(tokens, WIDE)
+    by_set = exchange(jnp.concatenate([by_head, key_part], axis=1), IZ)
+    owned = jnp.sum(by_set[:, :packed].astype(f32), axis=0).astype(bf16)
+    key_grad = jnp.sum(by_set[:, packed:].astype(f32), axis=0)
     value_grad = jnp.sum(value_parts.astype(f32), axis=0)
+    total = to_all(owned, "head")
+    d_lat = total[:, : SLABS * chunk].reshape(heads, SLABS, chunk, LANES)
+    d_rot = total[:, SLABS * chunk :].reshape(heads, chunk // 2, 2, ROPE_DIM)
+
+    def rows_of(grad):
+        return grad.reshape(HEADS_HERE, weight_rows, LANES).transpose(1, 0, 2).reshape(
+            weight_rows, HEADS_HERE * LANES
+        )
+
     return (
         d_nope,
         d_rope,
-        total[:, :LATENT],
-        total[:, LATENT : LATENT + ROPE_DIM],
-        key_grad,
-        value_grad,
+        d_lat.transpose(0, 2, 1, 3).reshape(tokens, LATENT),
+        d_rot.transpose(0, 2, 1, 3).reshape(tokens, ROPE_DIM),
+        rows_of(key_grad),
+        rows_of(value_grad),
     )
 
 

time: 186 us -> 180 us (0.968)
  waiting for transfers between devices: 67.5 us -> 64.3 us
  Pallas kernels: 41.7 us -> 39.2 us
  local copies, waits for them, and re-layouts: 7.83 us -> 10.1 us
  other arithmetic: 9.67 us -> 7.58 us
    ppermute x6, waiting for transfers between devices: 8.54 us -> 5.57 us  [to_partner(): return lax.ppermute(x, 'core', [(0, 1), (1, 0)])]
    pallas_call x1, Pallas kernels: 32.1 us -> 30.1 us  [local(): attend(block_order, ids, keys, q, g, row_vals, q_peer, g_peer, vals_peer)]
    unnamed x13 -> x18, local copies, waits for them, and re-layouts: 2.71 us -> 4.34 us
  transfers between devices with their start and end apart: 11 -> 11, of which waited for: 7 -> 6; matrix products, arithmetic and copies ran while one was open for 4% -> 4% of each run, Pallas kernels for 23% -> 22%
where the time goes in v4:
time: 180 us; the launch traced here: 177 us
  waiting for transfers between devices  64.3 us (36%)
  Pallas kernels  39.2 us (22%)
  starting transfers between devices  35.1 us (20%)
  blocking collectives  19.8 us (11%)
  local copies, waits for them, and re-layouts  10.1 us (6%)
  other arithmetic  7.58 us (4%)
    all_to_all x5, waiting for transfers between devices, exchange(): return lax.all_to_all(x, axis, split_axis=0, concat_axis=0, tiled=True)  58.7 us
    all_to_all x5, starting transfers between devices, exchange(): return lax.all_to_all(x, axis, split_axis=0, concat_axis=0, tiled=True)  34 us
    pallas_call x1, Pallas kernels, local(): attend(block_order, ids, keys, q, g, row_vals, q_peer, g_peer, vals_peer)  30.1 us
    all_to_all x1, blocking collectives, exchange(): return lax.all_to_all(x, axis, split_axis=0, concat_axis=0, tiled=True)  19.8 us
    ppermute x6, waiting for transfers between devices, to_partner(): return lax.ppermute(x, 'core', [(0, 1), (1, 0)])  5.57 us
    pallas_call x1, Pallas kernels, local(): pl.pallas_call(prepare_kernel, in_specs=in_smem(1) + in_vmem(6), out_spec...  5.04 us
    unnamed x18, local copies, waits for them, and re-layouts  4.34 us
    pallas_call x1, Pallas kernels, local(): pl.pallas_call(finish_kernel, in_specs=in_smem(1) + in_vmem(4), out_specs...  4.06 us
  transfers between devices with their start and end apart: 11, of which 6 were waited for; matrix products, arithmetic and copies ran while one was open for 4% of the time, Pallas kernels for 22%

profile of v4, /device:TPU:12, one launch (start us, length us, event | category | flops | bytes accessed | tf_op | source)
XLA Modules:
  0.0 176.9 jit_solution(1449526730819369571)
XLA Ops:
  1.3 0.9 constant_dynamic-slice_fusion
  2.4 0.7 constant_dynamic-update-slice_fusion.3
  4.6 19.8 %all_to_all.30 = bf16[16,72,128]{2,1,0:T(8,128)(2,1)S(1)} all-to-all(bf16[16,72,128]{2,1,0:T(8,128)(2,1)S(1)} %broadcast_in_dim.9), channel_id=1, replica_groups=mesh['head'=8,'inner'=2,'z'=8,'core'=2] {'inner','z'}, dimensions={0} | all-to-all | bytes 589824 | tf_op jit(solution)/shard_map/all_to_all | solution.py:191
  24.4 1.7 broadcast_in_dim.10
  26.1 7.3 %all-to-all-start.1 = ((bf16[8,16,72,128]{3,2,1,0:T(8,128)(2,1)}), bf16[8,16,72,128]{3,2,1,0:T(8,128)(2,1)S(1)}, u32[]{:S(2)}, u32[]{:S(2)}) async-start(bf16[8,16,72,128]{3,2,1,0:T(8,128)(2,1)} %broadcast_in_dim.10), calls=%async_computation.1 | async-start | bytes 4718592 | tf_op jit(solution)/shard_map/all_to_all | solution.py:191
  34.0 5.0 %prepare.1 = (bf16[2,512,640]{2,1,0:T(8,128)(2,1)}, bf16[2,512,512]{2,1,0:T(8,128)(2,1)}, f32[128,8]{1,0:T(8,128)}, f32[16,128,128]{2,1,0:T(8,128)}, bf16[16,128,128]{2,1,0:T(8,128)(2,1)}) custom-call(s32[2]{0:T(128)} %pad_add_fusion.ids, bf16[128,1024]{1,0:T(8,128)(2,1)} %nope.3, bf16[128,512]{1,0:T(8,128)(2,1)} %rope.1, bf16[512,1024]{1,0:T(8,128)(2,1)} %key_up.3, ...), custom_call_target="tpu_custom_call" | custom-call | tf_op jit(solution)/shard_map/prepare/pallas_call | solution.py:226
  39.7 0.9 copy.34
  41.2 3.4 %collective-permute-done.4 = bf16[16,128,128]{2,1,0:T(8,128)(2,1)} collective-permute-done((bf16[16,128,128]{2,1,0:T(8,128)(2,1)}, bf16[16,128,128]{2,1,0:T(8,128)(2,1)}, u32[]{:S(2)}, u32[]{:S(2)}) %collective-permute-start.4) | collective-permute-done | bytes 524320 | tf_op jit(solution)/shard_map/ppermute | solution.py:187
  44.6 2.3 %add_convert_fusion.1 = bf16[16,128,128]{2,1,0:T(8,128)(2,1)} fusion(f32[16,128,128]{2,1,0:T(8,128)} %get-tuple-element.29, bf16[16,128,128]{2,1,0:T(8,128)(2,1)} %collective-permute-done.4), kind=kLoop, calls=%fused_computation.3 | loop fusion | flops 786432 | bytes 2097152 | tf_op jit(solution)/shard_map/convert_element_type | solution.py:243
  47.0 12.4 %all-to-all-done.1.keys = bf16[8,16,72,128]{3,2,1,0:T(8,128)(2,1)S(1)} async-done(((bf16[8,16,72,128]{3,2,1,0:T(8,128)(2,1)}), bf16[8,16,72,128]{3,2,1,0:T(8,128)(2,1)S(1)}, u32[]{:S(2)}, u32[]{:S(2)}) %all-to-all-start.1) | async-done | bytes 2359328 | tf_op jit(solution)/shard_map/all_to_all | solution.py:191
  59.3 6.0 %all-to-all-start.2 = ((bf16[16,128,128]{2,1,0:T(8,128)(2,1)}), bf16[16,128,128]{2,1,0:T(8,128)(2,1)S(1)}, u32[]{:S(2)}, u32[]{:S(2)}) async-start(bf16[16,128,128]{2,1,0:T(8,128)(2,1)} %add_convert_fusion.1), calls=%async_computation.2 | async-start | bytes 1048576 | tf_op jit(solution)/shard_map/all_to_all | solution.py:191
  65.4 30.1 %attend.1 = (bf16[8,16,72,128]{3,2,1,0:T(8,128)(2,1)}, bf16[2,512,640]{2,1,0:T(8,128)(2,1)}, bf16[2,512,640]{2,1,0:T(8,128)(2,1)}) custom-call(s32[64]{0:T(128)} %order.1, s32[2]{0:T(128)} %pad_add_fusion.ids, bf16[8,16,72,128]{3,2,1,0:T(8,128)(2,1)} %copy-done, bf16[2,512,640]{2,1,0:T(8,128)(2,1)} %get-tuple-element.21.q0, ...), custom_call_target="tpu_custom_call" | custom-call | tf_op jit(solution)/shard_map/attend/pallas_call | solution.py:266
  95.5 6.3 %all-to-all-start.3 = ((bf16[8,16,72,128]{3,2,1,0:T(8,128)(2,1)}), bf16[8,16,72,128]{3,2,1,0:T(8,128)(2,1)S(1)}, u32[]{:S(2)}, u32[]{:S(2)}) async-start(bf16[8,16,72,128]{3,2,1,0:T(8,128)(2,1)} %get-tuple-element.32), calls=%async_computation.3 | async-start | bytes 4718592 | tf_op jit(solution)/shard_map/all_to_all | solution.py:191
  101.8 4.1 %finish.1 = (bf16[128,1024]{1,0:T(8,128)(2,1)}, bf16[128,512]{1,0:T(8,128)(2,1)}, f32[16,128,128]{2,1,0:T(8,128)}, bf16[16,128,128]{2,1,0:T(8,128)(2,1)}) custom-call(s32[2]{0:T(128)} %pad_add_fusion.ids, bf16[2,512,640]{2,1,0:T(8,128)(2,1)} %get-tuple-element.24.dq, bf16[2,512,640]{2,1,0:T(8,128)(2,1)} %collective-permute-done.3.dq_add, ...), custom_call_target="tpu_custom_call" | custom-call | tf_op jit(solution)/shard_map/finish/pallas_call | solution.py:270
  105.9 2.1 %collective-permute-done.5 = bf16[16,128,128]{2,1,0:T(8,128)(2,1)S(1)} collective-permute-done((bf16[16,128,128]{2,1,0:T(8,128)(2,1)}, bf16[16,128,128]{2,1,0:T(8,128)(2,1)S(1)}, u32[]{:S(2)}, u32[]{:S(2)}) %collective-permute-start.5) | collective-permute-done | bytes 524320 | tf_op jit(solution)/shard_map/ppermute | solution.py:187
  108.0 1.4 add_convert_fusion
  109.3 20.8 %all-to-all-done.3 = bf16[8,16,72,128]{3,2,1,0:T(8,128)(2,1)S(1)} async-done(((bf16[8,16,72,128]{3,2,1,0:T(8,128)(2,1)}), bf16[8,16,72,128]{3,2,1,0:T(8,128)(2,1)S(1)}, u32[]{:S(2)}, u32[]{:S(2)}) %all-to-all-start.3) | async-done | bytes 2359328 | tf_op jit(solution)/shard_map/all_to_all | solution.py:191
  130.1 1.1 reduce_sum.42
  131.3 1.9 %pad_maximum_fusion = bf16[16,200,128]{2,1,0:T(8,128)(2,1)} fusion(bf16[16,128,128]{2,1,0:T(8,128)(2,1)S(1)} %add_convert_fusion, bf16[16,72,128]{2,1,0:T(8,128)(2,1)} %reduce_sum.42), kind=kLoop, calls=%fused_computation.4 | loop fusion | flops 1638400 | bytes 1638400 | tf_op jit(solution)/shard_map/concatenate | solution.py:284
  133.2 8.1 %all-to-all-start.4 = ((bf16[16,200,128]{2,1,0:T(8,128)(2,1)}), bf16[16,200,128]{2,1,0:T(8,128)(2,1)S(1)}, u32[]{:S(2)}, u32[]{:S(2)}) async-start(bf16[16,200,128]{2,1,0:T(8,128)(2,1)} %pad_maximum_fusion), calls=%async_computation.4 | async-start | bytes 1638400 | tf_op jit(solution)/shard_map/all_to_all | solution.py:191
  142.0 21.6 %all-to-all-done.4 = bf16[16,200,128]{2,1,0:T(8,128)(2,1)S(1)} async-done(((bf16[16,200,128]{2,1,0:T(8,128)(2,1)}), bf16[16,200,128]{2,1,0:T(8,128)(2,1)S(1)}, u32[]{:S(2)}, u32[]{:S(2)}) %all-to-all-start.4) | async-done | bytes 819232 | tf_op jit(solution)/shard_map/all_to_all | solution.py:191
  164.4 6.3 %all-to-all-start.5 = ((bf16[8,72,128]{2,1,0:T(8,128)(2,1)}), bf16[8,72,128]{2,1,0:T(8,128)(2,1)S(1)}, u32[]{:S(2)}, u32[]{:S(2)}) async-start(bf16[8,72,128]{2,1,0:T(8,128)(2,1)} %broadcast_in_dim.11), calls=%async_computation.5 | async-start | bytes 294912 | tf_op jit(solution)/shard_map/all_to_all | solution.py:191
  171.4 3.9 %all-to-all-done.5 = bf16[8,72,128]{2,1,0:T(8,128)(2,1)S(1)} async-done(((bf16[8,72,128]{2,1,0:T(8,128)(2,1)}), bf16[8,72,128]{2,1,0:T(8,128)(2,1)S(1)}, u32[]{:S(2)}, u32[]{:S(2)}) %all-to-all-start.5) | async-done | bytes 147488 | tf_op jit(solution)/shard_map/all_to_all | solution.py:191
  176.2 0.7 copy.39
  (45 shorter events, 7.2 us)
Async XLA Ops:
  26.1 33.3 %all-to-all-start.1 = ((bf16[8,16,72,128]{3,2,1,0:T(8,128)(2,1)}), bf16[8,16,72,128]{3,2,1,0:T(8,128)(2,1)S(1)}, u32[]{:S(2)}, u32[]{:S(2)}) async-start(bf16[8,16,72,128]{3,2,1,0:T(8,128)(2,1)} %broadcast_in_dim.10), calls=%async_computation.1 | async-start | bytes 4718592 | tf_op jit(solution)/shard_map/all_to_all | solution.py:191
  34.0 5.6 %copy-start.4 = (f32[128,8]{0,1:T(8,128)S(1)}, f32[128,8]{0,1:T(8,128)}, u32[]{:S(2)}) copy-start(f32[128,8]{0,1:T(8,128)} %param.18) | copy-start | bytes 12292
  39.0 7.9 %collective-permute-start = (bf16[2,512,640]{2,1,0:T(8,128)(2,1)}, bf16[2,512,640]{2,1,0:T(8,128)(2,1)}, u32[]{:S(2)}, u32[]{:S(2)}) collective-permute-start(bf16[2,512,640]{2,1,0:T(8,128)(2,1)} %get-tuple-element.21.q0), channel_id=1, source_target_pairs={{0,1},{1,0},{2,3},{3,2},{4,5},{5,4},{6,7},{7,6},{8,9},{9,8},{10,11... | collective-permute-start | bytes 3932168 | tf_op jit(solution)/shard_map/ppermute | solution.py:187
  39.0 7.9 %collective-permute-start.1 = (bf16[2,512,512]{2,1,0:T(8,128)(2,1)}, bf16[2,512,512]{2,1,0:T(8,128)(2,1)S(1)}, u32[]{:S(2)}, u32[]{:S(2)}) collective-permute-start(bf16[2,512,512]{2,1,0:T(8,128)(2,1)} %get-tuple-element.22.g0), channel_id=1, source_target_pairs={{0,1},{1,0},{2,3},{3,2},{4,5},{5,4},{6,7},{7,6},{8,9},{9,8},{10,11... | collective-permute-start | bytes 3145736 | tf_op jit(solution)/shard_map/ppermute | solution.py:187
  39.5 5.1 %collective-permute-start.4 = (bf16[16,128,128]{2,1,0:T(8,128)(2,1)}, bf16[16,128,128]{2,1,0:T(8,128)(2,1)}, u32[]{:S(2)}, u32[]{:S(2)}) collective-permute-start(bf16[16,128,128]{2,1,0:T(8,128)(2,1)} %get-tuple-element.30), channel_id=1, source_target_pairs={{0,1},{1,0},{2,3},{3,2},{4,5},{5,4},{6,7},{7,6},{8,9},{9,8},{10,11... | collective-permute-start | bytes 1572872 | tf_op jit(solution)/shard_map/ppermute | solution.py:187
  40.7 24.6 %copy-start.2 = (f32[2,2,512]{2,1,0:T(2,128)}, f32[2,2,512]{2,1,0:T(2,128)S(1)}, u32[]{:S(2)}) copy-start(f32[2,2,512]{2,1,0:T(2,128)S(1)} %reshape.44.v0) | copy-start | bytes 24580
  40.7 6.2 %collective-permute-start.2 = (f32[2,2,512]{2,1,0:T(2,128)S(1)}, f32[2,2,512]{2,1,0:T(2,128)S(1)}, u32[]{:S(2)}, u32[]{:S(2)}) collective-permute-start(f32[2,2,512]{2,1,0:T(2,128)S(1)} %reshape.44.v0), channel_id=1, source_target_pairs={{0,1},{1,0},{2,3},{3,2},{4,5},{5,4},{6,7},{7,6},{8,9},{9,8},{10,11... | collective-permute-start | bytes 24584 | tf_op jit(solution)/shard_map/ppermute | solution.py:187
  46.9 18.4 %copy-start.3 = (f32[2,2,512]{2,1,0:T(2,128)}, f32[2,2,512]{2,1,0:T(2,128)S(1)}, u32[]{:S(2)}) copy-start(f32[2,2,512]{2,1,0:T(2,128)S(1)} %collective-permute-done.2.v1) | copy-start | bytes 24580
  47.0 12.4 %copy-start.1 = (bf16[2,512,512]{2,1,0:T(8,128)(2,1)}, bf16[2,512,512]{2,1,0:T(8,128)(2,1)S(1)}, u32[]{:S(2)}) copy-start(bf16[2,512,512]{2,1,0:T(8,128)(2,1)S(1)} %collective-permute-done.1.g1) | copy-start | bytes 3145732
  59.3 6.0 %copy-start = (bf16[8,16,72,128]{3,2,1,0:T(8,128)(2,1)}, bf16[8,16,72,128]{3,2,1,0:T(8,128)(2,1)S(1)}, u32[]{:S(2)}) copy-start(bf16[8,16,72,128]{3,2,1,0:T(8,128)(2,1)S(1)} %all-to-all-done.1.keys) | copy-start | bytes 7077892
  59.3 36.1 %all-to-all-start.2 = ((bf16[16,128,128]{2,1,0:T(8,128)(2,1)}), bf16[16,128,128]{2,1,0:T(8,128)(2,1)S(1)}, u32[]{:S(2)}, u32[]{:S(2)}) async-start(bf16[16,128,128]{2,1,0:T(8,128)(2,1)} %add_convert_fusion.1), calls=%async_computation.2 | async-start | bytes 1048576 | tf_op jit(solution)/shard_map/all_to_all | solution.py:191
  95.5 6.3 %collective-permute-start.3 = (bf16[2,512,640]{2,1,0:T(8,128)(2,1)}, bf16[2,512,640]{2,1,0:T(8,128)(2,1)}, u32[]{:S(2)}, u32[]{:S(2)}) collective-permute-start(bf16[2,512,640]{2,1,0:T(8,128)(2,1)} %get-tuple-element.25), channel_id=1, source_target_pairs={{0,1},{1,0},{2,3},{3,2},{4,5},{5,4},{6,7},{7,6},{8,9},{9,8},{10,11... | collective-permute-start | bytes 3932168 | tf_op jit(solution)/shard_map/ppermute | solution.py:187
  95.5 34.6 %all-to-all-start.3 = ((bf16[8,16,72,128]{3,2,1,0:T(8,128)(2,1)}), bf16[8,16,72,128]{3,2,1,0:T(8,128)(2,1)S(1)}, u32[]{:S(2)}, u32[]{:S(2)}) async-start(bf16[8,16,72,128]{3,2,1,0:T(8,128)(2,1)} %get-tuple-element.32), calls=%async_computation.3 | async-start | bytes 4718592 | tf_op jit(solution)/shard_map/all_to_all | solution.py:191
  105.9 2.1 %collective-permute-start.5 = (bf16[16,128,128]{2,1,0:T(8,128)(2,1)}, bf16[16,128,128]{2,1,0:T(8,128)(2,1)S(1)}, u32[]{:S(2)}, u32[]{:S(2)}) collective-permute-start(bf16[16,128,128]{2,1,0:T(8,128)(2,1)} %get-tuple-element.34), channel_id=1, source_target_pairs={{0,1},{1,0},{2,3},{3,2},{4,5},{5,4},{6,7},{7,6},{8,9},{9,8},{10,11... | collective-permute-start | bytes 1572872 | tf_op jit(solution)/shard_map/ppermute | solution.py:187
  133.2 30.5 %all-to-all-start.4 = ((bf16[16,200,128]{2,1,0:T(8,128)(2,1)}), bf16[16,200,128]{2,1,0:T(8,128)(2,1)S(1)}, u32[]{:S(2)}, u32[]{:S(2)}) async-start(bf16[16,200,128]{2,1,0:T(8,128)(2,1)} %pad_maximum_fusion), calls=%async_computation.4 | async-start | bytes 1638400 | tf_op jit(solution)/shard_map/all_to_all | solution.py:191
  164.4 10.9 %all-to-all-start.5 = ((bf16[8,72,128]{2,1,0:T(8,128)(2,1)}), bf16[8,72,128]{2,1,0:T(8,128)(2,1)S(1)}, u32[]{:S(2)}, u32[]{:S(2)}) async-start(bf16[8,72,128]{2,1,0:T(8,128)(2,1)} %broadcast_in_dim.11), calls=%async_computation.5 | async-start | bytes 294912 | tf_op jit(solution)/shard_map/all_to_all | solution.py:191

commit v5 on v4

--- a/solution.py
+++ b/solution.py
@@ -8,7 +8,6 @@
 LATENT = 512
 ROPE_DIM = 64
 NOPE_DIM = 128
-VALUE_DIM = 128
 WIDE = 640
 BLOCK = 64
 HEADS_HERE = 8
@@ -191,11 +190,27 @@
     return lax.all_to_all(x, axis, split_axis=0, concat_axis=0, tiled=True)
 
 
+def halved(parts):
+    bits = lax.axis_size("z").bit_length() - 1
+    left = parts.reshape((2,) * (1 + bits) + parts.shape[1:])
+    z = lax.axis_index("z")
+    for step in range(1 + bits):
+        axis, flip = ("inner", 1) if step == 0 else ("z", 1 << (step - 1))
+        bit = lax.axis_index("inner") if step == 0 else (z // flip) % 2
+        dim = 0 if step == 0 else bits - step
+        kept = lax.dynamic_index_in_dim(left, bit, dim, keepdims=False)
+        given = lax.dynamic_index_in_dim(left, 1 - bit, dim, keepdims=False)
+        pairs = [(i, i ^ flip) for i in range(lax.axis_size(axis))]
+        left = kept.astype(f32) + lax.ppermute(given, axis, pairs).astype(f32)
+        left = left.astype(bf16) if step < bits else left
+    return left
+
+
 def to_all(x, axis):
     return exchange(jnp.broadcast_to(x, (lax.axis_size(axis), *x.shape)), axis)
 
 
-def local(
+def whole(
     query_nope,
     query_rope,
     latent,
@@ -263,11 +278,14 @@
         compiler_params=params,
         name="attend",
     )
-    dk, dq, dq_give = attend(block_order, ids, keys, q, g, row_vals, q_peer, g_peer, vals_peer)
+    dk, dq, dq_give = attend(
+        block_order, ids, keys, q, g, row_vals, q_peer, g_peer, vals_peer
+    )
     dk, value_parts = lax.optimization_barrier((dk, value_parts))
-    by_head = jnp.sum(exchange(dk, "head").astype(f32), axis=0).astype(bf16)
+    from_heads = exchange(dk, "head")
+    by_head = jnp.sum(from_heads.astype(f32), axis=0).astype(bf16)
     dq_add = to_partner(dq_give)
-    d_nope, d_rope, key_keep, key_give = pl.pallas_call(
+    finish = pl.pallas_call(
         finish_kernel,
         in_specs=in_smem(1) + in_vmem(4),
         out_specs=in_vmem(4),
@@ -279,11 +297,11 @@
         ],
         compiler_params=params,
         name="finish",
-    )(ids, dq, dq_add, query_nope, key_up)
+    )
+    d_nope, d_rope, key_keep, key_give = finish(ids, dq, dq_add, query_nope, key_up)
     key_part = (key_keep + to_partner(key_give).astype(f32)).astype(bf16)
-    by_set = exchange(jnp.concatenate([by_head, key_part], axis=1), IZ)
-    owned = jnp.sum(by_set[:, :packed].astype(f32), axis=0).astype(bf16)
-    key_grad = jnp.sum(by_set[:, packed:].astype(f32), axis=0)
+    key_grad = halved(key_part)
+    owned = jnp.sum(exchange(by_head, IZ).astype(f32), axis=0).astype(bf16)
     value_grad = jnp.sum(value_parts.astype(f32), axis=0)
     total = to_all(owned, "head")
     d_lat = total[:, : SLABS * chunk].reshape(heads, SLABS, chunk, LANES)
@@ -311,7 +329,7 @@
     )
     rows = P(GRP, "head")
     return jax.shard_map(
-        local,
+        whole,
         mesh=fine,
         in_specs=(rows, rows, P(GRP, None), P(GRP, None), P(None, "head"), P(None, "head"),
                   rows, rows, rows, P()),

time: 180 us -> 197 us (1.094)
  blocking collectives: 19.8 us -> 41.2 us
  waiting for transfers between devices: 64.3 us -> 53.6 us
  local copies, waits for them, and re-layouts: 10.1 us -> 13.8 us
  starting transfers between devices: 35.1 us -> 38.6 us
    all_to_all x5 -> x4, waiting for transfers between devices: 58.7 us -> 18.6 us  [exchange(): return lax.all_to_all(x, axis, split_axis=0, concat_axis=0, tiled=True)]
    ppermute x0 -> x4, waiting for transfers between devices: none -> 29.5 us  [halved(): left = kept.astype(f32) + lax.ppermute(given, axis, pairs).astype(f32)]
    all_to_all x1 -> x2, blocking collectives: 19.8 us -> 41.2 us  [exchange(): return lax.all_to_all(x, axis, split_axis=0, concat_axis=0, tiled=True)]
    ppermute x0 -> x4, starting transfers between devices: none -> 11.3 us  [halved(): left = kept.astype(f32) + lax.ppermute(given, axis, pairs).astype(f32)]
    all_to_all x5 -> x4, starting transfers between devices: 34 us -> 26.1 us  [exchange(): return lax.all_to_all(x, axis, split_axis=0, concat_axis=0, tiled=True)]
    unnamed x18 -> x23, local copies, waits for them, and re-layouts: 4.34 us -> 7.87 us
    convert_element_type x2 -> x5, other arithmetic: 3.65 us -> 4.64 us  [the longest x3 1.98 us: halved(): left = left.astype(bf16) if step < bits else left]
  transfers between devices with their start and end apart: 11 -> 14, of which waited for: 6 -> 7; matrix products, arithmetic and copies ran while one was open for 4% -> 5% of each run, Pallas kernels for 22% -> 20%
where the time goes in v5:
time: 197 us; the launch traced here: 194 us
  waiting for transfers between devices  53.6 us (27%)
  blocking collectives  41.2 us (21%)
  Pallas kernels  39.2 us (20%)
  starting transfers between devices  38.6 us (20%)
  local copies, waits for them, and re-layouts  13.8 us (7%)
  other arithmetic  6.55 us (3%)
    all_to_all x2, blocking collectives, exchange(): return lax.all_to_all(x, axis, split_axis=0, concat_axis=0, tiled=True)  41.2 us
    pallas_call x1, Pallas kernels, whole(): attend(block_order, ids, keys, q, g, row_vals, q_peer, g_peer, vals_peer)  30.1 us
    ppermute x4, waiting for transfers between devices, halved(): left = kept.astype(f32) + lax.ppermute(given, axis, pairs).astype(f32)  29.5 us
    all_to_all x4, starting transfers between devices, exchange(): return lax.all_to_all(x, axis, split_axis=0, concat_axis=0, tiled=True)  26.1 us
    all_to_all x4, waiting for transfers between devices, exchange(): return lax.all_to_all(x, axis, split_axis=0, concat_axis=0, tiled=True)  18.6 us
    ppermute x4, starting transfers between devices, halved(): left = kept.astype(f32) + lax.ppermute(given, axis, pairs).astype(f32)  11.3 us
    unnamed x23, local copies, waits for them, and re-layouts  7.87 us
    ppermute x6, waiting for transfers between devices, to_partner(): return lax.ppermute(x, 'core', [(0, 1), (1, 0)])  5.56 us
  transfers between devices with their start and end apart: 14, of which 7 were waited for; matrix products, arithmetic and copies ran while one was open for 5% of the time, Pallas kernels for 20%

profile of v5, /device:TPU:12, one launch (start us, length us, event | category | flops | bytes accessed | tf_op | source)
XLA Modules:
  0.0 193.8 jit_solution(8121550858078464295)
XLA Ops:
  4.6 19.8 %all_to_all.30 = bf16[16,72,128]{2,1,0:T(8,128)(2,1)S(1)} all-to-all(bf16[16,72,128]{2,1,0:T(8,128)(2,1)S(1)} %broadcast_in_dim.9), channel_id=1, replica_groups=mesh['head'=8,'inner'=2,'z'=8,'core'=2] {'inner','z'}, dimensions={0} | all-to-all | bytes 589824 | tf_op jit(solution)/shard_map/all_to_all | solution.py:190
  24.4 1.7 broadcast_in_dim.10
  26.1 7.3 %all-to-all-start.1 = ((bf16[8,16,72,128]{3,2,1,0:T(8,128)(2,1)}), bf16[8,16,72,128]{3,2,1,0:T(8,128)(2,1)S(1)}, u32[]{:S(2)}, u32[]{:S(2)}) async-start(bf16[8,16,72,128]{3,2,1,0:T(8,128)(2,1)} %broadcast_in_dim.10), calls=%async_computation.1 | async-start | bytes 4718592 | tf_op jit(solution)/shard_map/all_to_all | solution.py:190
  34.0 5.0 %prepare.1 = (bf16[2,512,640]{2,1,0:T(8,128)(2,1)}, bf16[2,512,512]{2,1,0:T(8,128)(2,1)}, f32[128,8]{1,0:T(8,128)}, f32[16,128,128]{2,1,0:T(8,128)}, bf16[16,128,128]{2,1,0:T(8,128)(2,1)}) custom-call(s32[2]{0:T(128)} %pad_add_fusion.ids, bf16[128,1024]{1,0:T(8,128)(2,1)} %nope.3, bf16[128,512]{1,0:T(8,128)(2,1)} %rope.1, bf16[512,1024]{1,0:T(8,128)(2,1)} %key_up.3, ...), custom_call_target="tpu_custom_call" | custom-call | tf_op jit(solution)/shard_map/prepare/pallas_call | solution.py:241
  41.2 3.4 %collective-permute-done.2.v1 = f32[2,2,512]{2,1,0:T(2,128)S(1)} collective-permute-done((f32[2,2,512]{2,1,0:T(2,128)S(1)}, f32[2,2,512]{2,1,0:T(2,128)S(1)}, u32[]{:S(2)}, u32[]{:S(2)}) %collective-permute-start.2) | collective-permute-done | bytes 8224 | tf_op jit(solution)/shard_map/ppermute | solution.py:186
  44.6 14.7 %all-to-all-done.1.keys = bf16[8,16,72,128]{3,2,1,0:T(8,128)(2,1)S(1)} async-done(((bf16[8,16,72,128]{3,2,1,0:T(8,128)(2,1)}), bf16[8,16,72,128]{3,2,1,0:T(8,128)(2,1)S(1)}, u32[]{:S(2)}, u32[]{:S(2)}) %all-to-all-start.1) | async-done | bytes 2359328 | tf_op jit(solution)/shard_map/all_to_all | solution.py:190
  59.3 1.4 copy-done
  60.8 30.1 %attend.1 = (bf16[8,16,72,128]{3,2,1,0:T(8,128)(2,1)}, bf16[2,512,640]{2,1,0:T(8,128)(2,1)}, bf16[2,512,640]{2,1,0:T(8,128)(2,1)}) custom-call(s32[64]{0:T(128)} %order.1, s32[2]{0:T(128)} %pad_add_fusion.ids, bf16[8,16,72,128]{3,2,1,0:T(8,128)(2,1)} %copy-done, bf16[2,512,640]{2,1,0:T(8,128)(2,1)} %get-tuple-element.21.q0, ...), custom_call_target="tpu_custom_call" | custom-call | tf_op jit(solution)/shard_map/attend/pallas_call | solution.py:281
  90.9 1.2 add_convert_fusion.1
  92.0 21.4 %all_to_all.31 = bf16[16,128,128]{2,1,0:T(8,128)(2,1)S(1)} all-to-all(bf16[16,128,128]{2,1,0:T(8,128)(2,1)S(1)} %add_convert_fusion.1), channel_id=1, replica_groups=mesh['head'=8,'inner'=2,'z'=8,'core'=2] {'inner','z'}, dimensions={0} | all-to-all | bytes 1048576 | tf_op jit(solution)/shard_map/all_to_all | solution.py:190
  113.5 6.3 %all-to-all-start.3 = ((bf16[8,16,72,128]{3,2,1,0:T(8,128)(2,1)}), bf16[8,16,72,128]{3,2,1,0:T(8,128)(2,1)S(1)}, u32[]{:S(2)}, u32[]{:S(2)}) async-start(bf16[8,16,72,128]{3,2,1,0:T(8,128)(2,1)} %get-tuple-element.32), calls=%async_computation.3 | async-start | bytes 4718592 | tf_op jit(solution)/shard_map/all_to_all | solution.py:190
  119.8 4.1 %finish.1 = (bf16[128,1024]{1,0:T(8,128)(2,1)}, bf16[128,512]{1,0:T(8,128)(2,1)}, f32[16,128,128]{2,1,0:T(8,128)}, bf16[16,128,128]{2,1,0:T(8,128)(2,1)}) custom-call(s32[2]{0:T(128)} %pad_add_fusion.ids, bf16[2,512,640]{2,1,0:T(8,128)(2,1)} %get-tuple-element.24.dq, bf16[2,512,640]{2,1,0:T(8,128)(2,1)} %collective-permute-done.3.dq_add, ...), custom_call_target="tpu_custom_call" | custom-call | tf_op jit(solution)/shard_map/finish/pallas_call | solution.py:301
  123.9 2.1 %collective-permute-done.5 = bf16[16,128,128]{2,1,0:T(8,128)(2,1)S(1)} collective-permute-done((bf16[16,128,128]{2,1,0:T(8,128)(2,1)}, bf16[16,128,128]{2,1,0:T(8,128)(2,1)S(1)}, u32[]{:S(2)}, u32[]{:S(2)}) %collective-permute-start.5) | collective-permute-done | bytes 524320 | tf_op jit(solution)/shard_map/ppermute | solution.py:186
  126.8 1.5 add_convert_fusion
  130.0 20.0 %collective-permute-done.6 = bf16[2,2,2,128,128]{4,3,2,1,0:T(8,128)(2,1)} collective-permute-done((bf16[2,2,2,128,128]{4,3,2,1,0:T(8,128)(2,1)}, bf16[2,2,2,128,128]{4,3,2,1,0:T(8,128)(2,1)}, u32[]{:S(2)}, u32[]{:S(2)}) %collective-permute-start.6) | collective-permute-done | bytes 262176 | tf_op jit(solution)/shard_map/ppermute | solution.py:204
  151.8 3.3 %collective-permute-start.7 = (bf16[2,2,128,128]{3,2,1,0:T(8,128)(2,1)S(1)}, bf16[2,2,128,128]{3,2,1,0:T(8,128)(2,1)S(1)}, u32[]{:S(2)}, u32[]{:S(2)}) collective-permute-start(bf16[2,2,128,128]{3,2,1,0:T(8,128)(2,1)S(1)} %dynamic-slice_bitcast_fusion.1), channel_id=1, source_target_pairs={{0,2},{2,0},{4,6},{6,4},{8,10},{10,8},{12,14},{14,12},{1,3},{3,1},... | collective-permute-start | bytes 393224 | tf_op jit(solution)/shard_map/ppermute | solution.py:204
  155.0 2.9 %collective-permute-done.7 = bf16[2,2,128,128]{3,2,1,0:T(8,128)(2,1)S(1)} collective-permute-done((bf16[2,2,128,128]{3,2,1,0:T(8,128)(2,1)S(1)}, bf16[2,2,128,128]{3,2,1,0:T(8,128)(2,1)S(1)}, u32[]{:S(2)}, u32[]{:S(2)}) %collective-permute-start.7) | collective-permute-done | bytes 131104 | tf_op jit(solution)/shard_map/ppermute | solution.py:204
  158.9 1.1 reduce_sum.33
  160.0 5.3 %all-to-all-start.4 = ((bf16[16,72,128]{2,1,0:T(8,128)(2,1)}), bf16[16,72,128]{2,1,0:T(8,128)(2,1)S(1)}, u32[]{:S(2)}, u32[]{:S(2)}) async-start(bf16[16,72,128]{2,1,0:T(8,128)(2,1)} %reduce_sum.33), calls=%async_computation.4 | async-start | bytes 589824 | tf_op jit(solution)/shard_map/all_to_all | solution.py:190
  165.3 2.9 %collective-permute-start.8 = (bf16[2,128,128]{2,1,0:T(8,128)(2,1)S(1)}, bf16[2,128,128]{2,1,0:T(8,128)(2,1)S(1)}, u32[]{:S(2)}, u32[]{:S(2)}) collective-permute-start(bf16[2,128,128]{2,1,0:T(8,128)(2,1)S(1)} %dynamic-slice_bitcast_fusion.2), channel_id=1, source_target_pairs={{0,4},{2,6},{4,0},{6,2},{8,12},{10,14},{12,8},{14,10},{1,5},{3,7},... | collective-permute-start | bytes 196616 | tf_op jit(solution)/shard_map/ppermute | solution.py:204
  168.2 6.5 %collective-permute-done.8 = bf16[2,128,128]{2,1,0:T(8,128)(2,1)S(1)} collective-permute-done((bf16[2,128,128]{2,1,0:T(8,128)(2,1)S(1)}, bf16[2,128,128]{2,1,0:T(8,128)(2,1)S(1)}, u32[]{:S(2)}, u32[]{:S(2)}) %collective-permute-start.8) | collective-permute-done | bytes 65568 | tf_op jit(solution)/shard_map/ppermute | solution.py:204
  174.8 4.1 %collective-permute-start.9 = (bf16[128,128]{1,0:T(8,128)(2,1)S(1)}, bf16[128,128]{1,0:T(8,128)(2,1)S(1)}, u32[]{:S(2)}, u32[]{:S(2)}) collective-permute-start(bf16[128,128]{1,0:T(8,128)(2,1)S(1)} %dynamic-slice_bitcast_fusion.3), channel_id=1, source_target_pairs={{0,8},{2,10},{4,12},{6,14},{8,0},{10,2},{12,4},{14,6},{1,9},{3,11}... | collective-permute-start | bytes 98312 | tf_op jit(solution)/shard_map/ppermute | solution.py:204
  180.4 7.2 %all-to-all-start.5 = ((bf16[8,72,128]{2,1,0:T(8,128)(2,1)}), bf16[8,72,128]{2,1,0:T(8,128)(2,1)S(1)}, u32[]{:S(2)}, u32[]{:S(2)}) async-start(bf16[8,72,128]{2,1,0:T(8,128)(2,1)} %broadcast_in_dim.11), calls=%async_computation.5 | async-start | bytes 294912 | tf_op jit(solution)/shard_map/all_to_all | solution.py:190
  188.3 3.9 %all-to-all-done.5 = bf16[8,72,128]{2,1,0:T(8,128)(2,1)S(1)} async-done(((bf16[8,72,128]{2,1,0:T(8,128)(2,1)}), bf16[8,72,128]{2,1,0:T(8,128)(2,1)S(1)}, u32[]{:S(2)}, u32[]{:S(2)}) %all-to-all-start.5) | async-done | bytes 147488 | tf_op jit(solution)/shard_map/all_to_all | solution.py:190
  (63 shorter events, 15.7 us)
Async XLA Ops:
  26.1 33.3 %all-to-all-start.1 = ((bf16[8,16,72,128]{3,2,1,0:T(8,128)(2,1)}), bf16[8,16,72,128]{3,2,1,0:T(8,128)(2,1)S(1)}, u32[]{:S(2)}, u32[]{:S(2)}) async-start(bf16[8,16,72,128]{3,2,1,0:T(8,128)(2,1)} %broadcast_in_dim.10), calls=%async_computation.1 | async-start | bytes 4718592 | tf_op jit(solution)/shard_map/all_to_all | solution.py:190
  34.0 5.6 %copy-start.6 = (f32[128,8]{0,1:T(8,128)S(1)}, f32[128,8]{0,1:T(8,128)}, u32[]{:S(2)}) copy-start(f32[128,8]{0,1:T(8,128)} %param.18) | copy-start | bytes 12292
  39.0 5.6 %collective-permute-start = (bf16[2,512,640]{2,1,0:T(8,128)(2,1)}, bf16[2,512,640]{2,1,0:T(8,128)(2,1)}, u32[]{:S(2)}, u32[]{:S(2)}) collective-permute-start(bf16[2,512,640]{2,1,0:T(8,128)(2,1)} %get-tuple-element.21.q0), channel_id=1, source_target_pairs={{0,1},{1,0},{2,3},{3,2},{4,5},{5,4},{6,7},{7,6},{8,9},{9,8},{10,11... | collective-permute-start | bytes 3932168 | tf_op jit(solution)/shard_map/ppermute | solution.py:186
  39.0 5.6 %collective-permute-start.1 = (bf16[2,512,512]{2,1,0:T(8,128)(2,1)}, bf16[2,512,512]{2,1,0:T(8,128)(2,1)}, u32[]{:S(2)}, u32[]{:S(2)}) collective-permute-start(bf16[2,512,512]{2,1,0:T(8,128)(2,1)} %get-tuple-element.22.g0), channel_id=1, source_target_pairs={{0,1},{1,0},{2,3},{3,2},{4,5},{5,4},{6,7},{7,6},{8,9},{9,8},{10,11... | collective-permute-start | bytes 3145736 | tf_op jit(solution)/shard_map/ppermute | solution.py:186
  39.5 51.4 %collective-permute-start.4 = (bf16[16,128,128]{2,1,0:T(8,128)(2,1)}, bf16[16,128,128]{2,1,0:T(8,128)(2,1)}, u32[]{:S(2)}, u32[]{:S(2)}) collective-permute-start(bf16[16,128,128]{2,1,0:T(8,128)(2,1)} %get-tuple-element.30), channel_id=1, source_target_pairs={{0,1},{1,0},{2,3},{3,2},{4,5},{5,4},{6,7},{7,6},{8,9},{9,8},{10,11... | collective-permute-start | bytes 1572872 | tf_op jit(solution)/shard_map/ppermute | solution.py:186
  40.7 18.7 %copy-start.4 = (f32[2,2,512]{2,1,0:T(2,128)}, f32[2,2,512]{2,1,0:T(2,128)S(1)}, u32[]{:S(2)}) copy-start(f32[2,2,512]{2,1,0:T(2,128)S(1)} %reshape.55.v0) | copy-start | bytes 24580
  40.7 50.2 %copy-start.1 = (f32[16,128,128]{2,1,0:T(8,128)S(1)}, f32[16,128,128]{2,1,0:T(8,128)}, u32[]{:S(2)}) copy-start(f32[16,128,128]{2,1,0:T(8,128)} %get-tuple-element.29) | copy-start | bytes 3145732
  40.7 3.9 %collective-permute-start.2 = (f32[2,2,512]{2,1,0:T(2,128)S(1)}, f32[2,2,512]{2,1,0:T(2,128)S(1)}, u32[]{:S(2)}, u32[]{:S(2)}) collective-permute-start(f32[2,2,512]{2,1,0:T(2,128)S(1)} %reshape.55.v0), channel_id=1, source_target_pairs={{0,1},{1,0},{2,3},{3,2},{4,5},{5,4},{6,7},{7,6},{8,9},{9,8},{10,11... | collective-permute-start | bytes 24584 | tf_op jit(solution)/shard_map/ppermute | solution.py:186
  44.6 14.7 %copy-start.5 = (f32[2,2,512]{2,1,0:T(2,128)}, f32[2,2,512]{2,1,0:T(2,128)S(1)}, u32[]{:S(2)}) copy-start(f32[2,2,512]{2,1,0:T(2,128)S(1)} %collective-permute-done.2.v1) | copy-start | bytes 24580
  59.3 1.4 copy-start
  90.8 29.0 %collective-permute-start.3 = (bf16[2,512,640]{2,1,0:T(8,128)(2,1)}, bf16[2,512,640]{2,1,0:T(8,128)(2,1)}, u32[]{:S(2)}, u32[]{:S(2)}) collective-permute-start(bf16[2,512,640]{2,1,0:T(8,128)(2,1)} %get-tuple-element.25), channel_id=1, source_target_pairs={{0,1},{1,0},{2,3},{3,2},{4,5},{5,4},{6,7},{7,6},{8,9},{9,8},{10,11... | collective-permute-start | bytes 3932168 | tf_op jit(solution)/shard_map/ppermute | solution.py:186
  113.5 45.4 %all-to-all-start.3 = ((bf16[8,16,72,128]{3,2,1,0:T(8,128)(2,1)}), bf16[8,16,72,128]{3,2,1,0:T(8,128)(2,1)S(1)}, u32[]{:S(2)}, u32[]{:S(2)}) async-start(bf16[8,16,72,128]{3,2,1,0:T(8,128)(2,1)} %get-tuple-element.32), calls=%async_computation.3 | async-start | bytes 4718592 | tf_op jit(solution)/shard_map/all_to_all | solution.py:190
  123.9 2.1 %collective-permute-start.5 = (bf16[16,128,128]{2,1,0:T(8,128)(2,1)}, bf16[16,128,128]{2,1,0:T(8,128)(2,1)S(1)}, u32[]{:S(2)}, u32[]{:S(2)}) collective-permute-start(bf16[16,128,128]{2,1,0:T(8,128)(2,1)} %get-tuple-element.34), channel_id=1, source_target_pairs={{0,1},{1,0},{2,3},{3,2},{4,5},{5,4},{6,7},{7,6},{8,9},{9,8},{10,11... | collective-permute-start | bytes 1572872 | tf_op jit(solution)/shard_map/ppermute | solution.py:186
  126.0 0.8 copy-start.3
  129.0 21.0 %collective-permute-start.6 = (bf16[2,2,2,128,128]{4,3,2,1,0:T(8,128)(2,1)}, bf16[2,2,2,128,128]{4,3,2,1,0:T(8,128)(2,1)}, u32[]{:S(2)}, u32[]{:S(2)}) collective-permute-start(bf16[2,2,2,128,128]{4,3,2,1,0:T(8,128)(2,1)} %dynamic-slice_bitcast_fusion), channel_id=1, source_target_pairs={{0,16},{16,0},{1,17},{17,1},{2,18},{18,2},{3,19},{19,3},{4,20},{20... | collective-permute-start | bytes 786440 | tf_op jit(solution)/shard_map/ppermute | solution.py:204
  151.0 0.7 copy-start.2
  151.8 6.2 %collective-permute-start.7 = (bf16[2,2,128,128]{3,2,1,0:T(8,128)(2,1)S(1)}, bf16[2,2,128,128]{3,2,1,0:T(8,128)(2,1)S(1)}, u32[]{:S(2)}, u32[]{:S(2)}) collective-permute-start(bf16[2,2,128,128]{3,2,1,0:T(8,128)(2,1)S(1)} %dynamic-slice_bitcast_fusion.1), channel_id=1, source_target_pairs={{0,2},{2,0},{4,6},{6,4},{8,10},{10,8},{12,14},{14,12},{1,3},{3,1},... | collective-permute-start | bytes 393224 | tf_op jit(solution)/shard_map/ppermute | solution.py:204
  160.0 19.7 %all-to-all-start.4 = ((bf16[16,72,128]{2,1,0:T(8,128)(2,1)}), bf16[16,72,128]{2,1,0:T(8,128)(2,1)S(1)}, u32[]{:S(2)}, u32[]{:S(2)}) async-start(bf16[16,72,128]{2,1,0:T(8,128)(2,1)} %reduce_sum.33), calls=%async_computation.4 | async-start | bytes 589824 | tf_op jit(solution)/shard_map/all_to_all | solution.py:190
  165.3 9.4 %collective-permute-start.8 = (bf16[2,128,128]{2,1,0:T(8,128)(2,1)S(1)}, bf16[2,128,128]{2,1,0:T(8,128)(2,1)S(1)}, u32[]{:S(2)}, u32[]{:S(2)}) collective-permute-start(bf16[2,128,128]{2,1,0:T(8,128)(2,1)S(1)} %dynamic-slice_bitcast_fusion.2), channel_id=1, source_target_pairs={{0,4},{2,6},{4,0},{6,2},{8,12},{10,14},{12,8},{14,10},{1,5},{3,7},... | collective-permute-start | bytes 196616 | tf_op jit(solution)/shard_map/ppermute | solution.py:204
  174.8 12.8 %collective-permute-start.9 = (bf16[128,128]{1,0:T(8,128)(2,1)S(1)}, bf16[128,128]{1,0:T(8,128)(2,1)S(1)}, u32[]{:S(2)}, u32[]{:S(2)}) collective-permute-start(bf16[128,128]{1,0:T(8,128)(2,1)S(1)} %dynamic-slice_bitcast_fusion.3), channel_id=1, source_target_pairs={{0,8},{2,10},{4,12},{6,14},{8,0},{10,2},{12,4},{14,6},{1,9},{3,11}... | collective-permute-start | bytes 98312 | tf_op jit(solution)/shard_map/ppermute | solution.py:204
  180.4 11.8 %all-to-all-start.5 = ((bf16[8,72,128]{2,1,0:T(8,128)(2,1)}), bf16[8,72,128]{2,1,0:T(8,128)(2,1)S(1)}, u32[]{:S(2)}, u32[]{:S(2)}) async-start(bf16[8,72,128]{2,1,0:T(8,128)(2,1)} %broadcast_in_dim.11), calls=%async_computation.5 | async-start | bytes 294912 | tf_op jit(solution)/shard_map/all_to_all | solution.py:190
